TPU v7x, 256 devices: a whole 4x4x8 slice. The times are simulated.
256 devices in a mesh: ifg: 128 (over y, z_lo, x, core), slab: 2 (over z_hi).
Axes of the slice: x: 4, y: 4, z: 8 (z_hi: 2, z_lo: 4; z = z_hi * 4 + z_lo), core: 2. Of those that a mesh axis runs over, the one named last changes fastest.
Arguments:
- phase: float32 [2, 1152, 49152], P('slab', 'ifg'), may hold values from -60 to 60
- corrections: int32 [2, 1152, 49152], P('slab', 'ifg'), may hold values from -1 to 1
- closure_loops: int32 [288, 1152], replicated, may hold values from -1 to 1, as said below
- design: int32 [1152, 288], replicated, may hold values from -1 to 1, as said below
Outputs:
- closure_phase: float32 [2, 288, 49152], P('slab', None, 'ifg')
- displacement: float32 [2, 288, 49152], P('slab', None, 'ifg')
- misfit: float32 [2], P('slab')
Inputs may be any that keep to these rules, and one draw needn't show every extreme that they name: Each row of closure_loops holds +1 at two interferograms and -1 at a third; closure_loops times design is zero. Each row of design holds one +1 and one -1 in different columns; every date is named by some row.
All inputs are finite; a program needn't handle non-finite values.
Results may differ from a plain program's by a relative error of at most 0.0003.
Values sent between devices are 32-bit elements; how exact they have to be, the bound alone decides.
No kernel may reach another device: no remote copies, remote signals or barrier semaphores. Data moves between devices by JAX's collectives and lax.ppermute only.
A program may use at most 64 MiB of HBM per device.

v0:
```python
import functools

import jax
import jax.numpy as jnp
from jax import lax
from jax.experimental import pallas as pl
from jax.experimental.pallas import tpu as pltpu
from jax.sharding import Mesh
from jax.sharding import PartitionSpec as P

IFG = ("ifg_0", "ifg_1", "ifg_2", "ifg_3")
ALL = (*IFG, "slab")

ridge_weight = 1.0
two_pi = 6.283185307179586
epsilon = 1e-06
LANES = 128
VMEM = pl.BlockSpec(memory_space=pltpu.VMEM)
f32, bf16 = jnp.float32, jnp.bfloat16


def eye_mask(n):
    rows = lax.broadcasted_iota(jnp.int32, (n, n), 0)
    return rows == lax.broadcasted_iota(jnp.int32, (n, n), 1)


def head_kernel(parts, phase_ref, counts_ref, out_ref):
    rows, lines, _ = phase_ref.shape
    group = lines // parts
    for r in range(rows):
        for j in range(parts):
            at = pl.ds(j, group, stride=parts)
            out_ref[pl.ds(r * parts + j, group, stride=rows * parts), :] = phase_ref[
                r, at, :
            ] + two_pi * counts_ref[r, at, :].astype(f32)


def head(phase, counts, parts, steps):
    rows, lines, _ = phase.shape
    block = pl.BlockSpec((rows, lines // steps, LANES), lambda i: (0, i, 0))
    return pl.pallas_call(
        functools.partial(head_kernel, parts),
        grid=(steps,),
        in_specs=[block, block],
        out_specs=pl.BlockSpec((rows * lines // steps, LANES), lambda i: (i, 0)),
        out_shape=jax.ShapeDtypeStruct((rows * lines, LANES), f32),
        name="head",
    )(phase, counts)


def thirds(x):
    a = x.astype(bf16)
    rest = x - a.astype(f32)
    b = rest.astype(bf16)
    return a, b, (rest - b.astype(f32)).astype(bf16)


def exact_dot(left16, pieces):
    return sum(jnp.dot(left16, p, preferred_element_type=f32) for p in reversed(pieces))


def full_dot(left, right):
    a, b = thirds(left), thirds(right)
    pairs = ((0, 2), (2, 0), (1, 1), (0, 1), (1, 0), (0, 0))
    return sum(jnp.dot(a[i], b[j], preferred_element_type=f32) for i, j in pairs)


def prep_kernel(loops_ref, turned_ref, loops16_ref, design16_ref, turned16_ref, inverse_ref, power_ref):
    loops16_ref[...] = loops_ref[...].astype(f32).astype(bf16)
    turned = turned_ref[...].astype(f32)
    design16_ref[...] = turned.T.astype(bf16)
    turned16_ref[...] = turned.astype(bf16)
    eye = eye_mask(turned.shape[0])
    gram = jnp.dot(turned16_ref[...], design16_ref[...], preferred_element_type=f32)
    on_diagonal = jnp.where(eye, gram + ridge_weight, 0.0)
    column = jnp.sum(on_diagonal, axis=1, keepdims=True)
    row = jnp.sum(on_diagonal, axis=0, keepdims=True)
    step = jnp.where(eye, 0.0, -gram) / column
    power_ref[...] = step
    inverse_ref[...] = jnp.where(eye, 1.0, 0.0) + step

    def norm():
        return jnp.max(jnp.sum(power_ref[...], axis=1))

    def double(_):
        power = power_ref[...]
        power_ref[...] = full_dot(power, power)
        inverse_ref[...] += full_dot(inverse_ref[...], power_ref[...])
        return norm()

    lax.while_loop(lambda size: size > 1e-9, double, norm())
    inverse_ref[...] = inverse_ref[...] / row


def prep(loops, design):
    n, m = loops.shape
    dates = design.shape[1]
    return pl.pallas_call(
        prep_kernel,
        in_specs=[VMEM, VMEM],
        out_specs=[VMEM] * 4,
        out_shape=[
            jax.ShapeDtypeStruct((n, m), bf16),
            jax.ShapeDtypeStruct((m, dates), bf16),
            jax.ShapeDtypeStruct((dates, m), bf16),
            jax.ShapeDtypeStruct((dates, dates), f32),
        ],
        scratch_shapes=[pltpu.VMEM((dates, dates), f32)],
        name="prep",
    )(loops, design.T)


def copies_of(source_ref, held_ref, sems, chunks):
    rows = source_ref.shape[0] // chunks
    return [
        pltpu.make_async_copy(
            source_ref.at[pl.ds(k * rows, rows), :], held_ref.at[pl.ds(k * rows, rows), :], sems.at[k]
        )
        for k in range(chunks)
    ]


def side_by_side(held_ref, start, count, parts):
    return jnp.concatenate(
        [held_ref[pl.ds(start * parts + j, count, stride=parts), :] for j in range(parts)], axis=1
    )


def dates_kernel(parts, chunks, c_ref, design_ref, turned_ref, inverse_ref, shifts_ref, sums_ref, held_ref, sems):
    copies = copies_of(c_ref, held_ref, sems, chunks)
    for copy in copies:
        copy.start()
    ifgs, dates = design_ref.shape
    step = ifgs // chunks
    projected = 0.0
    for k in range(chunks):
        copies[k].wait()
        pieces = thirds(side_by_side(held_ref, k * step, step, parts))
        projected += exact_dot(turned_ref[:, k * step : (k + 1) * step], pieces)
    shifts = full_dot(inverse_ref[...], projected)
    shifts_ref[...] = shifts
    pieces = thirds(shifts)
    square = 0.0
    for k in range(chunks):
        model = exact_dot(design_ref[k * step : (k + 1) * step, :], pieces)
        residual = side_by_side(held_ref, k * step, step, parts) - model
        square += jnp.sum(residual * residual)
    ones = jnp.ones((8, shifts.shape[1]), bf16)
    sums_ref[:, :dates] = sum(
        lax.dot_general(ones, p, (((1,), (1,)), ((), ())), preferred_element_type=f32) for p in reversed(pieces)
    )
    sums_ref[:, dates:] = jnp.full((8, sums_ref.shape[1] - dates), square, f32)


def dates_part(c, design16, turned16, inverse, parts, width, chunks):
    dates = design16.shape[1]
    return pl.pallas_call(
        functools.partial(dates_kernel, parts, chunks),
        in_specs=[pl.BlockSpec(memory_space=pl.ANY)] + [VMEM] * 3,
        out_specs=[VMEM] * 2,
        out_shape=[
            jax.ShapeDtypeStruct((dates, parts * LANES), f32),
            jax.ShapeDtypeStruct((8, width), f32),
        ],
        scratch_shapes=[pltpu.VMEM(c.shape, f32), pltpu.SemaphoreType.DMA((chunks,))],
        name="dates",
    )(c, design16, turned16, inverse)


def loops_kernel(parts, chunks, c_ref, loops_ref, closure_ref, held_ref, sems):
    copies = copies_of(c_ref, held_ref, sems, chunks)
    for copy in copies:
        copy.start()
    step = loops_ref.shape[1] // chunks
    closure = 0.0
    for k in range(chunks):
        copies[k].wait()
        pieces = thirds(side_by_side(held_ref, k * step, step, parts))
        closure += exact_dot(loops_ref[:, k * step : (k + 1) * step], pieces)
    closure_ref[0] = closure


def loops_part(c, loops16, parts, chunks):
    return pl.pallas_call(
        functools.partial(loops_kernel, parts, chunks),
        in_specs=[pl.BlockSpec(memory_space=pl.ANY), VMEM],
        out_specs=VMEM,
        out_shape=jax.ShapeDtypeStruct((1, loops16.shape[0], parts * LANES), f32),
        scratch_shapes=[pltpu.VMEM(c.shape, f32), pltpu.SemaphoreType.DMA((chunks,))],
        name="loops",
    )(c, loops16)


def final_kernel(slabs, pixels, count, slab_ref, got_ref, shifts_ref, displacement_ref, misfit_ref):
    dates = displacement_ref.shape[1]
    got = got_ref[...]
    peers, width = got.shape
    total = jnp.sum(got[:, :dates], axis=0, keepdims=True) / (slabs * pixels)
    mine = lax.rem(lax.broadcasted_iota(jnp.int32, (peers, width - dates), 0), slabs) == slab_ref[0]
    square = jnp.sum(jnp.where(mine, got[:, dates:], 0.0), axis=0, keepdims=True)
    misfit_ref[...] = jnp.sqrt(square / count + epsilon)
    mean = jnp.sum(jnp.where(eye_mask(dates), total, 0.0), axis=1, keepdims=True)
    displacement_ref[0] = shifts_ref[...] - mean


def local(phase, corrections, closure_loops, design):
    slabs = lax.axis_size("slab")
    peers = lax.axis_size(IFG)
    rows, pixels = phase.shape[1:]
    parts = pixels // (peers * LANES)
    dates = design.shape[1]
    width = -(-(dates + 1) // LANES) * LANES
    lines = (rows, pixels // LANES, LANES)
    tiles = head(phase.reshape(lines), corrections.reshape(lines), parts, 8)
    got = lax.all_to_all(tiles.reshape(peers, 1, -1), IFG, split_axis=0, concat_axis=0, tiled=True)
    got = got.reshape(tiles.shape)
    loops16, design16, turned16, inverse = prep(closure_loops, design)
    shifts, sums = dates_part(got, design16, turned16, inverse, parts, width, 4)
    everyone = jnp.broadcast_to(sums[:1], (peers * slabs, 1, width))
    everyone = lax.all_to_all(everyone, ALL, split_axis=0, concat_axis=0, tiled=True)
    everyone = everyone.reshape(peers * slabs, width)
    closure = loops_part(got, loops16, parts, 4)
    displacement, misfit = pl.pallas_call(
        functools.partial(final_kernel, slabs, pixels, design.shape[0] * pixels),
        in_specs=[pl.BlockSpec(memory_space=pltpu.SMEM)] + [VMEM] * 2,
        out_specs=[VMEM] * 2,
        out_shape=[jax.ShapeDtypeStruct((1, dates, parts * LANES), f32), jax.ShapeDtypeStruct((1, width - dates), f32)],
        name="final",
    )(lax.axis_index("slab").reshape(1), everyone, shifts)
    return (closure, displacement, misfit[0, :1])


def solution(mesh):
    split = Mesh(
        mesh.devices.reshape(4, 4, 4, 2, mesh.shape["slab"]),
        (*IFG, "slab"),
    )
    in_specs = (P("slab", IFG, None), P("slab", IFG, None), P(), P())
    out_specs = (P("slab", None, IFG), P("slab", None, IFG), P("slab"))
    return jax.shard_map(local, mesh=split, in_specs=in_specs, out_specs=out_specs, check_vma=False)
```

profile of v0, /device:TPU:1, one launch (start us, length us, event | category | flops | bytes accessed | tf_op | source)
XLA Modules:
  0.0 106.6 jit_solution(13836480433755924127)
XLA Ops:
  0.6 6.1 %head.1 = f32[3456,128]{1,0:T(8,128)} custom-call(f32[9,384,128]{2,1,0:T(8,128)} %bitcast.14, s32[9,384,128]{2,1,0:T(8,128)} %bitcast.15), custom_call_target="tpu_custom_call" | custom-call | tf_op jit(solution)/shard_map/head/pallas_call | solution.py:41
  6.7 13.8 %all-to-all-start = ((f32[128,1,3456]{2,1,0:T(1,128)}), f32[128,1,3456]{2,1,0:T(1,128)S(1)}, u32[]{:S(2)}, u32[]{:S(2)}) async-start(f32[128,1,3456]{2,1,0:T(1,128)} %bitcast.13), calls=%async_computation | async-start | bytes 3538944 | tf_op jit(solution)/shard_map/all_to_all | solution.py:215
  20.5 22.4 %prep.1 = (bf16[288,1152]{1,0:T(8,128)(2,1)}, bf16[1152,288]{1,0:T(8,128)(2,1)}, bf16[288,1152]{1,0:T(8,128)(2,1)}, f32[288,288]{1,0:T(8,128)}) custom-call(s32[288,1152]{1,0:T(8,128)} %loops_ref.1, s32[288,1152]{1,0:T(8,128)} %bitcast.17), custom_call_target="tpu_custom_call" | custom-call | tf_op jit(solution)/shard_map/prep/pallas_call | solution.py:98
  42.9 22.5 %all-to-all-done = f32[128,1,3456]{2,1,0:T(1,128)S(1)} async-done(((f32[128,1,3456]{2,1,0:T(1,128)}), f32[128,1,3456]{2,1,0:T(1,128)S(1)}, u32[]{:S(2)}, u32[]{:S(2)}) %all-to-all-start) | async-done | bytes 1769504 | tf_op jit(solution)/shard_map/all_to_all | solution.py:215
  65.4 0.0 copy-start
  65.4 1.2 %copy-done = f32[128,1,3456]{2,1,0:T(1,128)} copy-done((f32[128,1,3456]{2,1,0:T(1,128)}, f32[128,1,3456]{2,1,0:T(1,128)S(1)}, u32[]{:S(2)}) %copy-start) | copy-done | bytes 1769496
  66.6 8.7 %dates.1 = (f32[288,384]{1,0:T(8,128)}, f32[8,384]{1,0:T(8,128)}) custom-call(f32[3456,128]{1,0:T(8,128)} %bitcast.11, bf16[1152,288]{1,0:T(8,128)(2,1)} %get-tuple-element.12.design_ref, bf16[288,1152]{1,0:T(8,128)(2,1)} %get-tuple-element.13.turned_ref, f32[288,288]{1,0:T(8,128)} %get-tuple-element.14.inverse_ref), custom_call_target="tpu_custom_call" | custom-call | tf_op jit(solution)/shard_map/dates/pallas_call | solution.py:157
  75.4 0.7 slice_reduce_fusion
  76.1 1.0 broadcast_in_dim.3
  77.1 8.7 %all-to-all-start.1 = ((f32[256,1,384]{2,1,0:T(1,128)}), f32[256,1,384]{2,1,0:T(1,128)S(1)}, u32[]{:S(2)}, u32[]{:S(2)}) async-start(f32[256,1,384]{2,1,0:T(1,128)} %broadcast_in_dim.3), calls=%async_computation.1 | async-start | bytes 786432 | tf_op jit(solution)/shard_map/all_to_all | solution.py:220
  85.8 5.4 %loops.1 = f32[1,288,384]{2,1,0:T(8,128)} custom-call(f32[3456,128]{1,0:T(8,128)} %bitcast.12, bf16[288,1152]{1,0:T(8,128)(2,1)} %get-tuple-element.11.loops_ref), custom_call_target="tpu_custom_call" | custom-call | tf_op jit(solution)/shard_map/loops/pallas_call | solution.py:184
  91.2 12.6 %all-to-all-done.1 = f32[256,1,384]{2,1,0:T(1,128)S(1)} async-done(((f32[256,1,384]{2,1,0:T(1,128)}), f32[256,1,384]{2,1,0:T(1,128)S(1)}, u32[]{:S(2)}, u32[]{:S(2)}) %all-to-all-start.1) | async-done | bytes 393248 | tf_op jit(solution)/shard_map/all_to_all | solution.py:220
  103.8 0.8 copy.10
  104.6 2.1 %final.1 = (f32[1,288,384]{2,1,0:T(8,128)}, f32[1,96]{1,0:T(1,128)}) custom-call(s32[1]{0:T(128)} %bitcast.5.slab_ref, f32[256,384]{1,0:T(8,128)} %bitcast.16, f32[288,384]{1,0:T(8,128)} %get-tuple-element.16.shifts_ref), custom_call_target="tpu_custom_call" | custom-call | tf_op jit(solution)/shard_map/final/pallas_call | solution.py:223
Async XLA Ops:
  6.7 58.7 %all-to-all-start = ((f32[128,1,3456]{2,1,0:T(1,128)}), f32[128,1,3456]{2,1,0:T(1,128)S(1)}, u32[]{:S(2)}, u32[]{:S(2)}) async-start(f32[128,1,3456]{2,1,0:T(1,128)} %bitcast.13), calls=%async_computation | async-start | bytes 3538944 | tf_op jit(solution)/shard_map/all_to_all | solution.py:215
  65.4 1.2 %copy-start = (f32[128,1,3456]{2,1,0:T(1,128)}, f32[128,1,3456]{2,1,0:T(1,128)S(1)}, u32[]{:S(2)}) copy-start(f32[128,1,3456]{2,1,0:T(1,128)S(1)} %all-to-all-done) | copy-start | bytes 5308420
  77.1 26.7 %all-to-all-start.1 = ((f32[256,1,384]{2,1,0:T(1,128)}), f32[256,1,384]{2,1,0:T(1,128)S(1)}, u32[]{:S(2)}, u32[]{:S(2)}) async-start(f32[256,1,384]{2,1,0:T(1,128)} %broadcast_in_dim.3), calls=%async_computation.1 | async-start | bytes 786432 | tf_op jit(solution)/shard_map/all_to_all | solution.py:220
where the time goes:
time: 107 us
  Pallas kernels  44.7 us (42%)
  waiting for transfers between devices  35 us (33%)
  starting transfers between devices  22.6 us (21%)
  local copies, waits for them, and re-layouts  3.68 us (3%)
    all_to_all x1, waiting for transfers between devices, local(): lax.all_to_all(tiles.reshape(peers, 1, -1), IFG, split_axis=0, concat_axi...  22.5 us
    pallas_call x1, Pallas kernels, prep(): pl.pallas_call(prep_kernel, in_specs=[VMEM, VMEM], out_specs=[VMEM] * 4,...  22.4 us
    all_to_all x1, starting transfers between devices, local(): lax.all_to_all(tiles.reshape(peers, 1, -1), IFG, split_axis=0, concat_axi...  13.8 us
    all_to_all x1, waiting for transfers between devices, local(): lax.all_to_all(everyone, ALL, split_axis=0, concat_axis=0, tiled=True)  12.6 us
    pallas_call x1, Pallas kernels, dates_part(): pl.pallas_call(functools.partial(dates_kernel, parts, chunks), in_specs=[...  8.74 us
    all_to_all x1, starting transfers between devices, local(): lax.all_to_all(everyone, ALL, split_axis=0, concat_axis=0, tiled=True)  8.73 us
    pallas_call x1, Pallas kernels, head(): pl.pallas_call(functools.partial(head_kernel, parts), grid=(steps,), in_s...  6.07 us
    pallas_call x1, Pallas kernels, loops_part(): pl.pallas_call(functools.partial(loops_kernel, parts, chunks), in_specs=[...  5.41 us
  transfers between devices with their start and end apart: 2, of which 2 were waited for; matrix products, arithmetic and copies ran while one was open for 0% of the time, Pallas kernels for 26%

commit v1 on v0

v1 whole, which is shorter than its diff:
```python
import functools

import jax
import jax.numpy as jnp
from jax import lax
from jax.experimental import pallas as pl
from jax.experimental.pallas import tpu as pltpu
from jax.sharding import Mesh
from jax.sharding import PartitionSpec as P

IFG = ("ifg_0", "ifg_1", "ifg_2", "ifg_3")

ridge_weight = 1.0
two_pi = 6.283185307179586
epsilon = 1e-06
LANES = 128
VMEM = pl.BlockSpec(memory_space=pltpu.VMEM)
ANY = pl.BlockSpec(memory_space=pl.ANY)
f32, bf16 = jnp.float32, jnp.bfloat16
PREP_VMEM = 66 * 1000 * 1000


def thirds(x):
    a = x.astype(bf16)
    rest = x - a.astype(f32)
    b = rest.astype(bf16)
    return a, b, (rest - b.astype(f32)).astype(bf16)


def exact_dot(left16, pieces):
    return sum(jnp.dot(left16, p, preferred_element_type=f32) for p in reversed(pieces))


def full_dot(left, right):
    a, b = thirds(left), thirds(right)
    pairs = ((0, 2), (2, 0), (1, 1), (0, 1), (1, 0), (0, 0))
    return sum(jnp.dot(a[i], b[j], preferred_element_type=f32) for i, j in pairs)


def head_kernel(parts, chunks, phase_ref, counts_ref, out_ref, phase_in, counts_in, sems):
    rows, lines, _ = phase_ref.shape
    peers = lines // parts
    span, group = lines // chunks, peers // chunks
    pitch = rows * parts + 1
    copies = []
    for k in range(chunks):
        at = pl.ds(k * span, span)
        for s, (a, b) in enumerate(((phase_ref, phase_in), (counts_ref, counts_in))):
            copies.append(pltpu.make_async_copy(a.at[:, at, :], b.at[:, at, :], sems.at[k, s]))
            copies[-1].start()
    sums = [jnp.zeros((8, LANES), f32) for _ in range(rows)]
    for k in range(chunks):
        copies[2 * k].wait()
        copies[2 * k + 1].wait()
        for r in range(rows):
            for j in range(parts):
                at = pl.ds(k * span + j, group, stride=parts)
                lines_in = phase_in[r, at, :] + two_pi * counts_in[r, at, :].astype(f32)
                out_ref[pl.ds(k * group * pitch + r * parts + j, group, stride=pitch), :] = lines_in
                sums[r] += jnp.sum(lines_in.reshape(group // 8, 8, LANES), axis=0)
    lane = lax.broadcasted_iota(jnp.int32, (1, LANES), 1)
    total = jnp.zeros((1, LANES), f32)
    for r in range(rows):
        total = jnp.where(lane == r, jnp.sum(sums[r], keepdims=True), total)
    out_ref[pl.ds(pitch - 1, peers, stride=pitch), :] = jnp.broadcast_to(total, (peers, LANES))


def head(phase, counts, parts, chunks):
    rows, lines, _ = phase.shape
    return pl.pallas_call(
        functools.partial(head_kernel, parts, chunks),
        in_specs=[ANY, ANY],
        out_specs=VMEM,
        out_shape=jax.ShapeDtypeStruct((lines // parts * (rows * parts + 1), LANES), f32),
        scratch_shapes=[
            pltpu.VMEM(phase.shape, f32),
            pltpu.VMEM(phase.shape, jnp.int32),
            pltpu.SemaphoreType.DMA((chunks, 2)),
        ],
        name="head",
    )(phase, counts)


def eye_mask(n):
    rows = lax.broadcasted_iota(jnp.int32, (n, n), 0)
    return rows == lax.broadcasted_iota(jnp.int32, (n, n), 1)


def prep_kernel(rows, loops_ref, turned_ref, loops16_ref, design16_ref, turned16_ref, inverse_ref, power_ref, tall_ref):
    ifgs = tall_ref.shape[0]
    peers = ifgs // rows
    for source, wide, tall in ((loops_ref, loops16_ref, None), (turned_ref, turned16_ref, design16_ref)):
        for start in range(0, source.shape[0], LANES):
            size = min(LANES, source.shape[0] - start)
            tall_ref[:, :size] = source[start : start + size, :].astype(f32).T
            for r in range(rows):
                some = tall_ref[pl.ds(r, peers, stride=rows), :]
                wide[start : start + size, r * peers : (r + 1) * peers] = some.T[:size].astype(bf16)
                if tall is not None:
                    tall[r * peers : (r + 1) * peers, start : start + size] = some[:, :size].astype(bf16)
    eye = eye_mask(turned_ref.shape[0])
    gram = jnp.dot(turned16_ref[...], design16_ref[...], preferred_element_type=f32)
    on_diagonal = jnp.where(eye, gram + ridge_weight, 0.0)
    column = jnp.sum(on_diagonal, axis=1, keepdims=True)
    row = jnp.sum(on_diagonal, axis=0, keepdims=True)
    step = jnp.where(eye, 0.0, -gram) / column
    power_ref[...] = step
    inverse_ref[...] = jnp.where(eye, 1.0, 0.0) + step

    def norm():
        return jnp.max(jnp.sum(power_ref[...], axis=1))

    def double(_):
        power = power_ref[...]
        power_ref[...] = full_dot(power, power)
        inverse_ref[...] += full_dot(inverse_ref[...], power_ref[...])
        return norm()

    lax.while_loop(lambda size: size > 1e-9, double, norm())
    inverse_ref[...] = inverse_ref[...] / row


def prep(loops, design, rows):
    n, m = loops.shape
    dates = design.shape[1]
    return pl.pallas_call(
        functools.partial(prep_kernel, rows),
        in_specs=[VMEM, VMEM],
        out_specs=[VMEM] * 4,
        out_shape=[
            jax.ShapeDtypeStruct((n, m), bf16),
            jax.ShapeDtypeStruct((m, dates), bf16),
            jax.ShapeDtypeStruct((dates, m), bf16),
            jax.ShapeDtypeStruct((dates, dates), f32),
        ],
        scratch_shapes=[pltpu.VMEM((dates, dates), f32), pltpu.VMEM((m, LANES), f32)],
        compiler_params=pltpu.CompilerParams(vmem_limit_bytes=PREP_VMEM),
        name="prep",
    )(loops, design.T)


def copies_of(source_ref, held_ref, sems, chunks):
    rows = source_ref.shape[0] // chunks
    return [
        pltpu.make_async_copy(
            source_ref.at[pl.ds(k * rows, rows), :], held_ref.at[pl.ds(k * rows, rows), :], sems.at[k]
        )
        for k in range(chunks)
    ]


def fetch(source_ref, held_ref, sems, chunks):
    copies = copies_of(source_ref, held_ref, sems, chunks)
    for copy in copies:
        copy.start()
    for copy in copies:
        copy.wait()


def lines_of(held_ref, r, parts, peers):
    pitch = held_ref.shape[0] // peers
    return jnp.concatenate(
        [held_ref[pl.ds(r * parts + j, peers, stride=pitch), :] for j in range(parts)], axis=1
    )


def dates_kernel(
    parts, rows, peers, chunks, c_ref, design_ref, turned_ref, inverse_ref, shifts_ref, square_ref, sums_ref, held_ref, sems
):
    fetch(c_ref, held_ref, sems, chunks)
    projected = 0.0
    for r in range(rows):
        pieces = thirds(lines_of(held_ref, r, parts, peers))
        projected += exact_dot(turned_ref[:, r * peers : (r + 1) * peers], pieces)
    shifts = full_dot(inverse_ref[...], projected)
    shifts_ref[...] = shifts
    pieces = thirds(shifts)[:2]
    square = 0.0
    for r in range(rows):
        model = exact_dot(design_ref[r * peers : (r + 1) * peers, :], pieces)
        residual = lines_of(held_ref, r, parts, peers) - model
        square += jnp.sum((residual * residual).reshape(peers // 8, 8, parts * LANES), axis=0)
    square_ref[...] = jnp.broadcast_to(jnp.sum(square, keepdims=True), square_ref.shape)
    pitch = held_ref.shape[0] // peers
    sums_ref[...] = held_ref[pl.ds(pitch - 1, peers, stride=pitch), :]


def dates_part(c, design16, turned16, inverse, parts, rows, peers, chunks):
    dates = design16.shape[1]
    return pl.pallas_call(
        functools.partial(dates_kernel, parts, rows, peers, chunks),
        in_specs=[ANY] + [VMEM] * 3,
        out_specs=[VMEM] * 3,
        out_shape=[
            jax.ShapeDtypeStruct((dates, parts * LANES), f32),
            jax.ShapeDtypeStruct((peers, LANES), f32),
            jax.ShapeDtypeStruct((peers, LANES), f32),
        ],
        scratch_shapes=[pltpu.VMEM(c.shape, f32), pltpu.SemaphoreType.DMA((chunks,))],
        name="dates",
    )(c, design16, turned16, inverse)


def loops_kernel(parts, rows, peers, chunks, c_ref, loops_ref, closure_ref, held_ref, sems):
    fetch(c_ref, held_ref, sems, chunks)
    closure = 0.0
    for r in range(rows):
        pieces = thirds(lines_of(held_ref, r, parts, peers))
        closure += exact_dot(loops_ref[:, r * peers : (r + 1) * peers], pieces)
    closure_ref[0] = closure


def loops_part(c, loops16, parts, rows, peers, chunks):
    return pl.pallas_call(
        functools.partial(loops_kernel, parts, rows, peers, chunks),
        in_specs=[ANY, VMEM],
        out_specs=VMEM,
        out_shape=jax.ShapeDtypeStruct((1, loops16.shape[0], parts * LANES), f32),
        scratch_shapes=[pltpu.VMEM(c.shape, f32), pltpu.SemaphoreType.DMA((chunks,))],
        name="loops",
    )(c, loops16)


def mean_kernel(rows, count, mine_ref, other_ref, turned_ref, inverse_ref, shifts_ref, displacement_ref):
    peers = mine_ref.shape[0]
    total = mine_ref[...] + other_ref[...]
    projected = 0.0
    for r in range(rows):
        column = jnp.broadcast_to(total[:, r : r + 1], (peers, LANES))
        projected += exact_dot(turned_ref[:, r * peers : (r + 1) * peers], thirds(column))
    mean = full_dot(inverse_ref[...], projected) / count
    for j in range(shifts_ref.shape[1] // LANES):
        at = slice(j * LANES, (j + 1) * LANES)
        displacement_ref[0, :, at] = shifts_ref[:, at] - mean


def mean_part(mine, other, turned16, inverse, shifts, rows, count):
    return pl.pallas_call(
        functools.partial(mean_kernel, rows, count),
        in_specs=[VMEM] * 5,
        out_specs=VMEM,
        out_shape=jax.ShapeDtypeStruct((1, *shifts.shape), f32),
        name="mean",
    )(mine, other, turned16, inverse, shifts)


def local(phase, corrections, closure_loops, design):
    slabs = lax.axis_size("slab")
    peers = lax.axis_size(IFG)
    rows, pixels = phase.shape[1:]
    parts = pixels // (peers * LANES)
    lines = (rows, pixels // LANES, LANES)
    tiles = head(phase.reshape(lines), corrections.reshape(lines), parts, 4)
    got = lax.all_to_all(tiles.reshape(peers, 1, -1), IFG, split_axis=0, concat_axis=0, tiled=True)
    got = got.reshape(tiles.shape)
    loops16, design16, turned16, inverse = prep(closure_loops, design, rows)
    shifts, square, sums = dates_part(got, design16, turned16, inverse, parts, rows, peers, 4)
    squares = lax.all_to_all(
        square.reshape(peers, 1, LANES), IFG, split_axis=0, concat_axis=0, tiled=True
    )
    other = lax.ppermute(sums, "slab", [(i, (i + 1) % slabs) for i in range(slabs)])
    closure = loops_part(got, loops16, parts, rows, peers, 4)
    displacement = mean_part(sums, other, turned16, inverse, shifts, rows, slabs * pixels)
    slab_square = jnp.sum(squares, axis=0)[0, :1]
    misfit = jnp.sqrt(slab_square / (design.shape[0] * pixels) + epsilon)
    return (closure, displacement, misfit)


def solution(mesh):
    split = Mesh(
        mesh.devices.reshape(4, 4, 4, 2, mesh.shape["slab"]),
        (*IFG, "slab"),
    )
    in_specs = (P("slab", IFG, None), P("slab", IFG, None), P(), P())
    out_specs = (P("slab", None, IFG), P("slab", None, IFG), P("slab"))
    return jax.shard_map(local, mesh=split, in_specs=in_specs, out_specs=out_specs, check_vma=False)
```

time: 107 us -> 95.4 us (0.89)
  waiting for transfers between devices: 35 us -> 22.1 us
  local copies, waits for them, and re-layouts: 3.68 us -> 0.62 us
  starting transfers between devices: 22.6 us -> 25.1 us
  between operations: 0.67 us -> 1.9 us
    all_to_all x1, waiting for transfers between devices: 12.6 us -> 0.01 us  [local(): lax.all_to_all(square.reshape(peers, 1, LANES), IFG, split_axis=0, concat...]
    ppermute x0 -> x1, starting transfers between devices: none -> 4.48 us  [local(): lax.ppermute(sums, 'slab', [(i, (i + 1) % slabs) for i in range(slabs)])]
    all_to_all x1, starting transfers between devices: 8.73 us -> 6.37 us  [local(): lax.all_to_all(square.reshape(peers, 1, LANES), IFG, split_axis=0, concat...]
    unnamed x3 -> x2, local copies, waits for them, and re-layouts: 2 us -> 0.62 us
  transfers between devices with their start and end apart: 2 -> 3, of which waited for: 2 -> 1; matrix products, arithmetic and copies ran while one was open for 0% -> 0% of each run, Pallas kernels for 26% -> 35%
where the time goes in v1:
time: 95.4 us; the launch traced here: 94.9 us
  Pallas kernels  45 us (47%)
  starting transfers between devices  25.1 us (26%)
  waiting for transfers between devices  22.1 us (23%)
  between operations  1.9 us (2%)
    pallas_call x1, Pallas kernels, prep(): pl.pallas_call(functools.partial(prep_kernel, rows), in_specs=[VMEM, VMEM...  23.8 us
    all_to_all x1, waiting for transfers between devices, local(): lax.all_to_all(tiles.reshape(peers, 1, -1), IFG, split_axis=0, concat_axi...  22.1 us
    all_to_all x1, starting transfers between devices, local(): lax.all_to_all(tiles.reshape(peers, 1, -1), IFG, split_axis=0, concat_axi...  14.2 us
    pallas_call x1, Pallas kernels, dates_part(): pl.pallas_call(functools.partial(dates_kernel, parts, rows, peers, chunks...  8.66 us
    all_to_all x1, starting transfers between devices, local(): lax.all_to_all(square.reshape(peers, 1, LANES), IFG, split_axis=0, concat...  6.37 us
    pallas_call x1, Pallas kernels, loops_part(): pl.pallas_call(functools.partial(loops_kernel, parts, rows, peers, chunks...  5.02 us
    ppermute x1, starting transfers between devices, local(): lax.ppermute(sums, 'slab', [(i, (i + 1) % slabs) for i in range(slabs)])  4.48 us
    pallas_call x1, Pallas kernels, mean_part(): pl.pallas_call(functools.partial(mean_kernel, rows, count), in_specs=[VME...  4.05 us
  transfers between devices with their start and end apart: 3, of which 1 were waited for; matrix products, arithmetic and copies ran while one was open for 0% of the time, Pallas kernels for 35%

profile of v1, /device:TPU:1, one launch (start us, length us, event | category | flops | bytes accessed | tf_op | source)
XLA Modules:
  0.0 94.9 jit_solution(17710044632848316187)
XLA Ops:
  0.6 3.5 %head.1 = f32[3584,128]{1,0:T(8,128)} custom-call(f32[9,384,128]{2,1,0:T(8,128)} %bitcast.12, s32[9,384,128]{2,1,0:T(8,128)} %bitcast.13), custom_call_target="tpu_custom_call" | custom-call | tf_op jit(solution)/shard_map/head/pallas_call | solution.py:70
  4.1 14.2 %all-to-all-start = ((f32[128,1,3584]{2,1,0:T(1,128)}), f32[128,1,3584]{2,1,0:T(1,128)}, u32[]{:S(2)}, u32[]{:S(2)}) async-start(f32[128,1,3584]{2,1,0:T(1,128)} %bitcast.11), calls=%async_computation | async-start | bytes 3670016 | tf_op jit(solution)/shard_map/all_to_all | solution.py:254
  18.3 23.8 %prep.1 = (bf16[288,1152]{1,0:T(8,128)(2,1)}, bf16[1152,288]{1,0:T(8,128)(2,1)}, bf16[288,1152]{1,0:T(8,128)(2,1)}, f32[288,288]{1,0:T(8,128)}) custom-call(s32[288,1152]{1,0:T(8,128)} %loops_ref.1, s32[288,1152]{1,0:T(8,128)} %bitcast.14), custom_call_target="tpu_custom_call" | custom-call | tf_op jit(solution)/shard_map/prep/pallas_call | solution.py:126
  42.2 22.1 %all-to-all-done = f32[128,1,3584]{2,1,0:T(1,128)} async-done(((f32[128,1,3584]{2,1,0:T(1,128)}), f32[128,1,3584]{2,1,0:T(1,128)}, u32[]{:S(2)}, u32[]{:S(2)}) %all-to-all-start) | async-done | bytes 1835040 | tf_op jit(solution)/shard_map/all_to_all | solution.py:254
  64.3 8.7 %dates.1 = (f32[288,384]{1,0:T(8,128)}, f32[128,128]{1,0:T(8,128)}, f32[128,128]{1,0:T(8,128)}) custom-call(f32[3584,128]{1,0:T(8,128)} %bitcast.3.c_ref, bf16[1152,288]{1,0:T(8,128)(2,1)} %get-tuple-element.11.design_ref, bf16[288,1152]{1,0:T(8,128)(2,1)} %get-tuple-element.12.turned_ref, f32[288,288]{1,0:T(8,128)} %get-tuple-element.13.inverse_ref), custom_call_target="tpu_custom_call" | custom-call | tf_op jit(solution)/shard_map/dates/pallas_call | solution.py:190
  73.0 6.4 %all-to-all-start.1 = ((f32[128,1,128]{2,1,0:T(1,128)}), f32[128,1,128]{2,1,0:T(1,128)S(1)}, u32[]{:S(2)}, u32[]{:S(2)}) async-start(f32[128,1,128]{2,1,0:T(1,128)} %bitcast.15), calls=%async_computation.1 | async-start | bytes 131072 | tf_op jit(solution)/shard_map/all_to_all | solution.py:258
  79.4 4.5 %collective-permute-start = (f32[128,128]{1,0:T(8,128)}, f32[128,128]{1,0:T(8,128)S(1)}, u32[]{:S(2)}, u32[]{:S(2)}) collective-permute-start(f32[128,128]{1,0:T(8,128)} %get-tuple-element.14.mine_ref), channel_id=1, source_target_pairs={{0,1},{1,0},{2,3},{3,2},{4,5},{5,4},{6,7},{7,6},{8,9},{9,8},{10,11... | collective-permute-start | bytes 196616 | tf_op jit(solution)/shard_map/ppermute | solution.py:261
  83.9 5.0 %loops.1 = f32[1,288,384]{2,1,0:T(8,128)} custom-call(f32[3584,128]{1,0:T(8,128)} %bitcast.3.c_ref, bf16[288,1152]{1,0:T(8,128)(2,1)} %get-tuple-element.10.loops_ref), custom_call_target="tpu_custom_call" | custom-call | tf_op jit(solution)/shard_map/loops/pallas_call | solution.py:214
  88.9 0.0 collective-permute-done.other_ref
  88.9 0.0 copy-start
  88.9 0.6 copy-done
  89.5 4.1 %mean.1 = f32[1,288,384]{2,1,0:T(8,128)} custom-call(f32[128,128]{1,0:T(8,128)} %get-tuple-element.14.mine_ref, f32[128,128]{1,0:T(8,128)} %copy-done, bf16[288,1152]{1,0:T(8,128)(2,1)} %get-tuple-element.12.turned_ref, f32[288,288]{1,0:T(8,128)} %get-tuple-element.13.inverse_ref, f32[288,384]{1,0:T(8,128)} %get-tuple-element.15.shifts_ref), custom_call_target="tpu_custom_call" | custom-call | tf_op jit(solution)/shard_map/mean/pallas_call | solution.py:238
  93.6 0.0 all-to-all-done.1
  93.6 0.2 reduce_sum.11
Async XLA Ops:
  4.1 60.2 %all-to-all-start = ((f32[128,1,3584]{2,1,0:T(1,128)}), f32[128,1,3584]{2,1,0:T(1,128)}, u32[]{:S(2)}, u32[]{:S(2)}) async-start(f32[128,1,3584]{2,1,0:T(1,128)} %bitcast.11), calls=%async_computation | async-start | bytes 3670016 | tf_op jit(solution)/shard_map/all_to_all | solution.py:254
  73.0 20.6 %all-to-all-start.1 = ((f32[128,1,128]{2,1,0:T(1,128)}), f32[128,1,128]{2,1,0:T(1,128)S(1)}, u32[]{:S(2)}, u32[]{:S(2)}) async-start(f32[128,1,128]{2,1,0:T(1,128)} %bitcast.15), calls=%async_computation.1 | async-start | bytes 131072 | tf_op jit(solution)/shard_map/all_to_all | solution.py:258
  79.4 9.5 %collective-permute-start = (f32[128,128]{1,0:T(8,128)}, f32[128,128]{1,0:T(8,128)S(1)}, u32[]{:S(2)}, u32[]{:S(2)}) collective-permute-start(f32[128,128]{1,0:T(8,128)} %get-tuple-element.14.mine_ref), channel_id=1, source_target_pairs={{0,1},{1,0},{2,3},{3,2},{4,5},{5,4},{6,7},{7,6},{8,9},{9,8},{10,11... | collective-permute-start | bytes 196616 | tf_op jit(solution)/shard_map/ppermute | solution.py:261
  88.9 0.6 copy-start

commit v2 on v1

v2 whole, which is shorter than its diff:
```python
import functools

import jax
import jax.numpy as jnp
from jax import lax
from jax.experimental import pallas as pl
from jax.experimental.pallas import tpu as pltpu
from jax.sharding import Mesh
from jax.sharding import PartitionSpec as P


IFG = ("ifg_0", "ifg_1", "ifg_2", "ifg_3")

ridge_weight = 1.0
two_pi = 6.283185307179586
epsilon = 1e-06
LANES = 128
VMEM = pl.BlockSpec(memory_space=pltpu.VMEM)
HBM = pl.BlockSpec(memory_space=pltpu.HBM)
SMEM = pl.BlockSpec(memory_space=pltpu.SMEM)
f32, bf16 = jnp.float32, jnp.bfloat16
SMALL = pltpu.CompilerParams(vmem_limit_bytes=16 * 2**20)


def in_hbm(x):
    return pltpu.with_memory_space_constraint(x, pltpu.HBM)


def thirds(x):
    a = x.astype(bf16)
    rest = x - a.astype(f32)
    b = rest.astype(bf16)
    return a, b, (rest - b.astype(f32)).astype(bf16)


PAIRS = ((0, 0), (0, 1), (0, 2), (1, 0), (1, 1), (2, 0))


def stack_right(stack_ref, x):
    pieces = thirds(x)
    n = x.shape[0]
    for k, (_, j) in enumerate(PAIRS):
        stack_ref[k * n : (k + 1) * n, :] = pieces[j]


def side_by_side(wide_ref, at, x):
    n = x.shape[1]
    for k, piece in enumerate(thirds(x)):
        wide_ref[at, k * n : (k + 1) * n] = piece


def folded(wide, count):
    n = wide.shape[1] // count
    return sum(wide[:, k * n : (k + 1) * n] for k in reversed(range(count)))


def head_kernel(parts, chunks, phase_ref, counts_ref, out_ref, sums_ref, phase_in, counts_in, sems):
    rows, lines, _ = phase_ref.shape
    peers = lines // parts
    span, group = lines // chunks, peers // chunks
    pitch = rows * parts
    copies = []
    for k in range(chunks):
        at = pl.ds(k * span, span)
        for s, (a, b) in enumerate(((phase_ref, phase_in), (counts_ref, counts_in))):
            copies.append(pltpu.make_async_copy(a.at[:, at, :], b.at[:, at, :], sems.at[k, s]))
            copies[-1].start()
    sums = [jnp.zeros((8, LANES), f32) for _ in range(rows)]
    for k in range(chunks):
        copies[2 * k].wait()
        copies[2 * k + 1].wait()
        for r in range(rows):
            for j in range(parts):
                at = pl.ds(k * span + j, group, stride=parts)
                some = phase_in[r, at, :] + two_pi * counts_in[r, at, :].astype(f32)
                out_ref[pl.ds(k * group * pitch + r * parts + j, group, stride=pitch), :] = some
                sums[r] += jnp.sum(some.reshape(group // 8, 8, LANES), axis=0)
    lane = lax.broadcasted_iota(jnp.int32, (1, LANES), 1)
    total = jnp.zeros((1, LANES), f32)
    for r in range(rows):
        total = jnp.where(lane == r + 1, jnp.sum(sums[r], keepdims=True), total)
    sums_ref[...] = jnp.broadcast_to(total, sums_ref.shape)


def head(phase, counts, parts, chunks):
    rows, lines, _ = phase.shape
    return pl.pallas_call(
        functools.partial(head_kernel, parts, chunks),
        in_specs=[HBM, HBM],
        out_specs=[VMEM, VMEM],
        out_shape=[pltpu.HBM((lines * rows, LANES), f32), jax.ShapeDtypeStruct((8, LANES), f32)],
        scratch_shapes=[
            pltpu.VMEM(phase.shape, f32),
            pltpu.VMEM(phase.shape, jnp.int32),
            pltpu.SemaphoreType.DMA((chunks, 2)),
        ],
        name="head",
    )(in_hbm(phase), in_hbm(counts))


def eye_mask(n):
    rows = lax.broadcasted_iota(jnp.int32, (n, n), 0)
    return rows == lax.broadcasted_iota(jnp.int32, (n, n), 1)


def doubled(left_ref, right_ref, power_ref, total_ref):
    n = power_ref.shape[0]
    power, total = power_ref[...], total_ref[...]
    stack_right(right_ref, power)
    for half, x in enumerate((power, total)):
        pieces = thirds(x)
        for k, (i, _) in enumerate(PAIRS):
            left_ref[half * n : (half + 1) * n, k * n : (k + 1) * n] = pieces[i]
    both = jnp.dot(left_ref[...], right_ref[...], preferred_element_type=f32)
    power_ref[...] = both[:n]
    total_ref[...] = total + both[n:]


def prep_kernel(
    rows, loops_ref, turned_ref, loops16_ref, design16_ref, turned16_ref, six_ref, direct_ref,
    tall_ref, power_ref, total_ref, left_ref, right_ref,
):
    peers = tall_ref.shape[0] // rows
    for source, wide, tall in ((loops_ref, loops16_ref, None), (turned_ref, turned16_ref, design16_ref)):
        for start in range(0, source.shape[0], LANES):
            size = min(LANES, source.shape[0] - start)
            tall_ref[:, :size] = source[start : start + size, :].astype(f32).T
            for r in range(rows):
                some = tall_ref[pl.ds(r, peers, stride=rows), :]
                wide[start : start + size, r * peers : (r + 1) * peers] = some.T[:size].astype(bf16)
                if tall is not None:
                    tall[r * peers : (r + 1) * peers, start : start + size] = some[:, :size].astype(bf16)
    eye = eye_mask(turned_ref.shape[0])
    gram = jnp.dot(turned16_ref[...], design16_ref[...], preferred_element_type=f32)
    on_diagonal = jnp.where(eye, gram + ridge_weight, 0.0)
    column = jnp.sum(on_diagonal, axis=1, keepdims=True)
    row = jnp.sum(on_diagonal, axis=0, keepdims=True)
    power_ref[...] = jnp.where(eye, 0.0, -gram) / column
    total_ref[...] = jnp.where(eye, 1.0, 0.0)

    def norm():
        return jnp.max(jnp.sum(power_ref[...], axis=1))

    def double(_):
        doubled(left_ref, right_ref, power_ref, total_ref)
        return norm()

    lax.while_loop(lambda size: size > 3e-8, double, norm())
    pieces = thirds(total_ref[...] / row)
    n = total_ref.shape[0]
    for k, (i, _) in enumerate(PAIRS):
        six_ref[:, k * n : (k + 1) * n] = pieces[i]
    direct_ref[...] = sum(jnp.dot(p, turned16_ref[...], preferred_element_type=f32) for p in reversed(pieces))


def prep(loops, design, rows):
    n, m = loops.shape
    dates = design.shape[1]
    return pl.pallas_call(
        functools.partial(prep_kernel, rows),
        in_specs=[VMEM, VMEM],
        out_specs=[VMEM] * 5,
        out_shape=[
            pltpu.HBM((n, m), bf16),
            pltpu.HBM((m, dates), bf16),
            pltpu.HBM((dates, m), bf16),
            pltpu.HBM((dates, dates * len(PAIRS)), bf16),
            pltpu.HBM((dates, m), f32),
        ],
        scratch_shapes=[
            pltpu.VMEM((m, LANES), f32),
            pltpu.VMEM((dates, dates), f32),
            pltpu.VMEM((dates, dates), f32),
            pltpu.VMEM((2 * dates, dates * len(PAIRS)), bf16),
            pltpu.VMEM((dates * len(PAIRS), dates), bf16),
        ],
        compiler_params=SMALL,
        name="prep",
    )(loops, design.T)


def lines_of(held_ref, r, parts, peers):
    pitch = held_ref.shape[0] // peers
    return jnp.concatenate(
        [held_ref[pl.ds(r * parts + j, peers, stride=pitch), :] for j in range(parts)], axis=1
    )


def dates_kernel(
    parts, rows, peers, held_ref, mine_ref, other_ref, turned_hbm, six_hbm, design_hbm, shifts_ref, line_ref,
    turned_ref, six_ref, design_ref, wide_ref, stack_ref, sems,
):
    copies = [
        pltpu.make_async_copy(turned_hbm, turned_ref, sems.at[0]),
        pltpu.make_async_copy(six_hbm, six_ref, sems.at[1]),
        pltpu.make_async_copy(design_hbm, design_ref, sems.at[2]),
    ]
    for copy in copies:
        copy.start()
    for r in range(rows):
        side_by_side(wide_ref, slice(r * peers, (r + 1) * peers), lines_of(held_ref, r, parts, peers))
    copies[0].wait()
    projected = folded(jnp.dot(turned_ref[...], wide_ref[...], preferred_element_type=f32), 3)
    stack_right(stack_ref, projected)
    copies[1].wait()
    shifts = jnp.dot(six_ref[...], stack_ref[...], preferred_element_type=f32)
    shifts_ref[...] = shifts
    two = jnp.concatenate(thirds(shifts)[:2], axis=1)
    copies[2].wait()
    square = 0.0
    for r in range(rows):
        model = folded(jnp.dot(design_ref[r * peers : (r + 1) * peers, :], two, preferred_element_type=f32), 2)
        residual = lines_of(held_ref, r, parts, peers) - model
        square += jnp.sum((residual * residual).reshape(peers // 8, 8, parts * LANES), axis=0)
    lane = lax.broadcasted_iota(jnp.int32, (1, LANES), 1)
    line = jnp.where(lane == 0, jnp.sum(square, keepdims=True), mine_ref[:1] + other_ref[:1])
    line_ref[...] = jnp.broadcast_to(line, line_ref.shape)


def dates_part(c, turned16, mine, other, design16, six, parts, rows, peers):
    ifgs, dates = design16.shape
    return pl.pallas_call(
        functools.partial(dates_kernel, parts, rows, peers),
        in_specs=[VMEM] * 3 + [HBM] * 3,
        out_specs=[VMEM] * 2,
        out_shape=[
            jax.ShapeDtypeStruct((dates, parts * LANES), f32),
            pltpu.HBM((peers, LANES), f32),
        ],
        scratch_shapes=[
            pltpu.VMEM(turned16.shape, bf16),
            pltpu.VMEM(six.shape, bf16),
            pltpu.VMEM(design16.shape, bf16),
            pltpu.VMEM((ifgs, 3 * parts * LANES), bf16),
            pltpu.VMEM((dates * len(PAIRS), parts * LANES), bf16),
            pltpu.SemaphoreType.DMA((3,)),
        ],
        compiler_params=SMALL,
        name="dates",
    )(c, mine, other, in_hbm(turned16), in_hbm(six), in_hbm(design16))


def loops_kernel(parts, rows, peers, held_ref, loops_hbm, closure_ref, loops_ref, wide_ref, sem):
    copy = pltpu.make_async_copy(loops_hbm, loops_ref, sem)
    copy.start()
    for r in range(rows):
        side_by_side(wide_ref, slice(r * peers, (r + 1) * peers), lines_of(held_ref, r, parts, peers))
    copy.wait()
    closure_ref[0] = folded(jnp.dot(loops_ref[...], wide_ref[...], preferred_element_type=f32), 3)


def loops_part(c, loops16, parts, rows, peers):
    return pl.pallas_call(
        functools.partial(loops_kernel, parts, rows, peers),
        in_specs=[VMEM, HBM],
        out_specs=VMEM,
        out_shape=jax.ShapeDtypeStruct((1, loops16.shape[0], parts * LANES), f32),
        scratch_shapes=[
            pltpu.VMEM(loops16.shape, bf16),
            pltpu.VMEM((loops16.shape[1], 3 * parts * LANES), bf16),
            pltpu.SemaphoreType.DMA,
        ],
        compiler_params=SMALL,
        name="loops",
    )(c, in_hbm(loops16))


def last_kernel(rows, count, squares, got_ref, direct_ref, shifts_ref, displacement_ref, misfit_ref):
    by_lane = got_ref[...].T
    square = jnp.sum(by_lane[:1], axis=1, keepdims=True)
    misfit_ref[...] = jnp.broadcast_to(jnp.sqrt(square / squares + epsilon), misfit_ref.shape)
    line = jnp.concatenate([by_lane[r + 1 : r + 2] for r in range(rows)], axis=1)
    mean = jnp.sum(direct_ref[...] * line, axis=1, keepdims=True) / count
    displacement_ref[0] = shifts_ref[...] - mean


def last_part(got, direct, shifts, rows, count, squares):
    return pl.pallas_call(
        functools.partial(last_kernel, rows, count, squares),
        in_specs=[VMEM] * 3,
        out_specs=[VMEM] * 2,
        out_shape=[
            jax.ShapeDtypeStruct((1, *shifts.shape), f32),
            jax.ShapeDtypeStruct((1, LANES), f32),
        ],
        compiler_params=SMALL,
        name="last",
    )(got, direct, shifts)


def local(phase, corrections, closure_loops, design):
    slabs = lax.axis_size("slab")
    peers = lax.axis_size(IFG)
    rows, pixels = phase.shape[1:]
    parts = pixels // (peers * LANES)
    lines = (rows, pixels // LANES, LANES)
    tiles, mine = head(phase.reshape(lines), corrections.reshape(lines), parts, 4)
    got = lax.all_to_all(tiles.reshape(peers, 1, -1), IFG, split_axis=0, concat_axis=0, tiled=True)
    got = got.reshape(tiles.shape)
    other = lax.ppermute(mine, "slab", [(i, (i + 1) % slabs) for i in range(slabs)])
    loops16, design16, turned16, six, direct = prep(closure_loops, design, rows)
    shifts, line = dates_part(got, turned16, mine, other, design16, six, parts, rows, peers)
    totals = lax.all_to_all(line.reshape(peers, 1, LANES), IFG, split_axis=0, concat_axis=0, tiled=True)
    closure = loops_part(got, loops16, parts, rows, peers)
    displacement, misfit = last_part(
        totals.reshape(peers, LANES), direct, shifts, rows, slabs * pixels, design.shape[0] * pixels
    )
    return (closure, displacement, misfit[0, :1])


def solution(mesh):
    split = Mesh(
        mesh.devices.reshape(4, 4, 4, 2, mesh.shape["slab"]),
        (*IFG, "slab"),
    )
    in_specs = (P("slab", IFG, None), P("slab", IFG, None), P(), P())
    out_specs = (P("slab", None, IFG), P("slab", None, IFG), P("slab"))
    return jax.shard_map(local, mesh=split, in_specs=in_specs, out_specs=out_specs, check_vma=False)
```

time: 95.4 us -> 87.6 us (0.918)
  Pallas kernels: 45 us -> 31 us
  waiting for transfers between devices: 22.1 us -> 28.4 us
  between operations: 1.9 us -> 0.71 us
    all_to_all x1, waiting for transfers between devices: 22.1 us -> 12.6 us  [local(): lax.all_to_all(tiles.reshape(peers, 1, -1), IFG, split_axis=0, concat_axi...]
    ppermute x1, waiting for transfers between devices: 0.01 us -> 8.9 us  [local(): lax.ppermute(mine, 'slab', [(i, (i + 1) % slabs) for i in range(slabs)])]
    pallas_call x4, Pallas kernels: 21.2 us -> 13.1 us  [the longest x1 4.97 us: dates_part(): pl.pallas_call(functools.partial(dates_kernel, parts, rows, peers), in_sp...]
    all_to_all x1, waiting for transfers between devices: 0.01 us -> 6.88 us  [local(): lax.all_to_all(line.reshape(peers, 1, LANES), IFG, split_axis=0, concat_a...]
    pallas_call x1, Pallas kernels: 23.8 us -> 17.9 us  [prep(): pl.pallas_call(functools.partial(prep_kernel, rows), in_specs=[VMEM, VMEM...]
    all_to_all x1, starting transfers between devices: 6.37 us -> 7.53 us  [local(): lax.all_to_all(line.reshape(peers, 1, LANES), IFG, split_axis=0, concat_a...]
  transfers between devices with their start and end apart: 3 -> 3, of which waited for: 1 -> 3; matrix products, arithmetic and copies ran while one was open for 0% -> 0% of each run, Pallas kernels for 35% -> 24%
where the time goes in v2:
time: 87.6 us; the launch traced here: 87.2 us
  Pallas kernels  31 us (35%)
  waiting for transfers between devices  28.4 us (32%)
  starting transfers between devices  25.8 us (29%)
  local copies, waits for them, and re-layouts  1.34 us (2%)
    pallas_call x1, Pallas kernels, prep(): pl.pallas_call(functools.partial(prep_kernel, rows), in_specs=[VMEM, VMEM...  17.9 us
    all_to_all x1, starting transfers between devices, local(): lax.all_to_all(tiles.reshape(peers, 1, -1), IFG, split_axis=0, concat_axi...  14 us
    all_to_all x1, waiting for transfers between devices, local(): lax.all_to_all(tiles.reshape(peers, 1, -1), IFG, split_axis=0, concat_axi...  12.6 us
    ppermute x1, waiting for transfers between devices, local(): lax.ppermute(mine, 'slab', [(i, (i + 1) % slabs) for i in range(slabs)])  8.9 us
    all_to_all x1, starting transfers between devices, local(): lax.all_to_all(line.reshape(peers, 1, LANES), IFG, split_axis=0, concat_a...  7.53 us
    all_to_all x1, waiting for transfers between devices, local(): lax.all_to_all(line.reshape(peers, 1, LANES), IFG, split_axis=0, concat_a...  6.88 us
    pallas_call x1, Pallas kernels, dates_part(): pl.pallas_call(functools.partial(dates_kernel, parts, rows, peers), in_sp...  4.97 us
    ppermute x1, starting transfers between devices, local(): lax.ppermute(mine, 'slab', [(i, (i + 1) % slabs) for i in range(slabs)])  4.3 us
  transfers between devices with their start and end apart: 3, of which 3 were waited for; matrix products, arithmetic and copies ran while one was open for 0% of the time, Pallas kernels for 24%

profile of v2, /device:TPU:1, one launch (start us, length us, event | category | flops | bytes accessed | tf_op | source)
XLA Modules:
  0.0 87.2 jit_solution(14448183912694308863)
XLA Ops:
  0.6 3.3 %head.1 = (f32[3456,128]{1,0:T(8,128)}, f32[8,128]{1,0:T(8,128)}) custom-call(f32[9,384,128]{2,1,0:T(8,128)} %bitcast.14, s32[9,384,128]{2,1,0:T(8,128)} %bitcast.15), custom_call_target="tpu_custom_call" | custom-call | tf_op jit(solution)/shard_map/head/pallas_call | solution.py:87
  3.9 0.0 copy-start.3
  4.0 0.0 copy-start.1
  4.0 14.0 %all-to-all-start = ((f32[128,1,3456]{2,1,0:T(1,128)}), f32[128,1,3456]{2,1,0:T(1,128)S(1)}, u32[]{:S(2)}, u32[]{:S(2)}) async-start(f32[128,1,3456]{2,1,0:T(1,128)} %bitcast.16), calls=%async_computation | async-start | bytes 3538944 | tf_op jit(solution)/shard_map/all_to_all | solution.py:298
  17.9 0.0 copy-done.3
  18.0 4.3 %collective-permute-start = (f32[8,128]{1,0:T(8,128)S(1)}, f32[8,128]{1,0:T(8,128)S(1)}, u32[]{:S(2)}, u32[]{:S(2)}) collective-permute-start(f32[8,128]{1,0:T(8,128)S(1)} %copy-done.3), channel_id=1, source_target_pairs={{0,1},{1,0},{2,3},{3,2},{4,5},{5,4},{6,7},{7,6},{8,9},{9,8},{10,11... | collective-permute-start | bytes 12296 | tf_op jit(solution)/shard_map/ppermute | solution.py:300
  22.3 0.0 copy-done.1
  22.3 0.0 copy-start.2
  22.3 1.3 %copy-done.2 = s32[1152,288]{0,1:T(8,128)S(1)} copy-done((s32[1152,288]{0,1:T(8,128)S(1)}, s32[1152,288]{0,1:T(8,128)}, u32[]{:S(2)}) %copy-start.2) | copy-done | bytes 1327128
  23.6 17.9 %prep.1 = (bf16[288,1152]{1,0:T(8,128)(2,1)}, bf16[1152,288]{1,0:T(8,128)(2,1)}, bf16[288,1152]{1,0:T(8,128)(2,1)}, bf16[288,1728]{1,0:T(8,128)(2,1)}, f32[288,1152]{1,0:T(8,128)}) custom-call(s32[288,1152]{1,0:T(8,128)S(1)} %copy-done.1, s32[288,1152]{1,0:T(8,128)S(1)} %bitcast.13), custom_call_target="tpu_custom_call" | custom-call | tf_op jit(solution)/shard_map/prep/pallas_call | solution.py:159
  41.5 8.9 %collective-permute-done.other_ref = f32[8,128]{1,0:T(8,128)S(1)} collective-permute-done((f32[8,128]{1,0:T(8,128)S(1)}, f32[8,128]{1,0:T(8,128)S(1)}, u32[]{:S(2)}, u32[]{:S(2)}) %collective-permute-start) | collective-permute-done | bytes 4128 | tf_op jit(solution)/shard_map/ppermute | solution.py:300
  50.4 12.6 %all-to-all-done = f32[128,1,3456]{2,1,0:T(1,128)S(1)} async-done(((f32[128,1,3456]{2,1,0:T(1,128)}), f32[128,1,3456]{2,1,0:T(1,128)S(1)}, u32[]{:S(2)}, u32[]{:S(2)}) %all-to-all-start) | async-done | bytes 1769504 | tf_op jit(solution)/shard_map/all_to_all | solution.py:298
  63.0 5.0 %dates.1 = (f32[288,384]{1,0:T(8,128)S(1)}, f32[128,128]{1,0:T(8,128)}) custom-call(f32[3456,128]{1,0:T(8,128)S(1)} %bitcast.11, f32[8,128]{1,0:T(8,128)S(1)} %copy-done.3, f32[8,128]{1,0:T(8,128)S(1)} %collective-permute-done.other_ref, bf16[288,1152]{1,0:T(8,128)(2,1)} %get-tuple-element.17.turned_hbm, bf16[288,1728]{1,0:T(8,128)(2,1)} %get-tuple-element.18.six_hbm, ...), custom_call_target="tpu_custom_call" | custom-call | tf_op jit(solution)/shard_map/dates/pallas_call | solution.py:222
  68.0 0.0 copy-start
  68.0 7.5 %all-to-all-start.1 = ((f32[128,1,128]{2,1,0:T(1,128)}), f32[128,1,128]{2,1,0:T(1,128)}, u32[]{:S(2)}, u32[]{:S(2)}) async-start(f32[128,1,128]{2,1,0:T(1,128)} %bitcast.17), calls=%async_computation.1 | async-start | bytes 131072 | tf_op jit(solution)/shard_map/all_to_all | solution.py:303
  75.5 3.0 %loops.1 = f32[1,288,384]{2,1,0:T(8,128)} custom-call(f32[3456,128]{1,0:T(8,128)S(1)} %bitcast.12, bf16[288,1152]{1,0:T(8,128)(2,1)} %get-tuple-element.15.loops_hbm), custom_call_target="tpu_custom_call" | custom-call | tf_op jit(solution)/shard_map/loops/pallas_call | solution.py:253
  78.5 6.9 %all-to-all-done.1 = f32[128,1,128]{2,1,0:T(1,128)} async-done(((f32[128,1,128]{2,1,0:T(1,128)}), f32[128,1,128]{2,1,0:T(1,128)}, u32[]{:S(2)}, u32[]{:S(2)}) %all-to-all-start.1) | async-done | bytes 65568 | tf_op jit(solution)/shard_map/all_to_all | solution.py:303
  85.4 0.0 copy-done
  85.4 1.8 %last.1 = (f32[1,288,384]{2,1,0:T(8,128)}, f32[1,128]{1,0:T(1,128)}) custom-call(f32[128,128]{1,0:T(8,128)} %bitcast.7.got_ref, f32[288,1152]{1,0:T(8,128)S(1)} %copy-done, f32[288,384]{1,0:T(8,128)S(1)} %get-tuple-element.22.shifts_ref), custom_call_target="tpu_custom_call" | custom-call | tf_op jit(solution)/shard_map/last/pallas_call | solution.py:278
Async XLA Ops:
  3.9 14.0 %copy-start.3 = (f32[8,128]{1,0:T(8,128)S(1)}, f32[8,128]{1,0:T(8,128)}, u32[]{:S(2)}) copy-start(f32[8,128]{1,0:T(8,128)} %get-tuple-element.16.mine_ref) | copy-start | bytes 12292
  4.0 18.3 %copy-start.1 = (s32[288,1152]{1,0:T(8,128)S(1)}, s32[288,1152]{1,0:T(8,128)}, u32[]{:S(2)}) copy-start(s32[288,1152]{1,0:T(8,128)} %loops_ref.1) | copy-start | bytes 3981316
  4.0 59.0 %all-to-all-start = ((f32[128,1,3456]{2,1,0:T(1,128)}), f32[128,1,3456]{2,1,0:T(1,128)S(1)}, u32[]{:S(2)}, u32[]{:S(2)}) async-start(f32[128,1,3456]{2,1,0:T(1,128)} %bitcast.16), calls=%async_computation | async-start | bytes 3538944 | tf_op jit(solution)/shard_map/all_to_all | solution.py:298
  18.0 32.5 %collective-permute-start = (f32[8,128]{1,0:T(8,128)S(1)}, f32[8,128]{1,0:T(8,128)S(1)}, u32[]{:S(2)}, u32[]{:S(2)}) collective-permute-start(f32[8,128]{1,0:T(8,128)S(1)} %copy-done.3), channel_id=1, source_target_pairs={{0,1},{1,0},{2,3},{3,2},{4,5},{5,4},{6,7},{7,6},{8,9},{9,8},{10,11... | collective-permute-start | bytes 12296 | tf_op jit(solution)/shard_map/ppermute | solution.py:300
  22.3 1.3 %copy-start.2 = (s32[1152,288]{0,1:T(8,128)S(1)}, s32[1152,288]{0,1:T(8,128)}, u32[]{:S(2)}) copy-start(s32[1152,288]{0,1:T(8,128)} %param.7) | copy-start | bytes 3981316
  68.0 17.4 %copy-start = (f32[288,1152]{1,0:T(8,128)S(1)}, f32[288,1152]{1,0:T(8,128)}, u32[]{:S(2)}) copy-start(f32[288,1152]{1,0:T(8,128)} %get-tuple-element.21.direct_ref) | copy-start | bytes 3981316
  68.0 17.4 %all-to-all-start.1 = ((f32[128,1,128]{2,1,0:T(1,128)}), f32[128,1,128]{2,1,0:T(1,128)}, u32[]{:S(2)}, u32[]{:S(2)}) async-start(f32[128,1,128]{2,1,0:T(1,128)} %bitcast.17), calls=%async_computation.1 | async-start | bytes 131072 | tf_op jit(solution)/shard_map/all_to_all | solution.py:303

commit v3 on v2

--- a/solution.py
+++ b/solution.py
@@ -117,21 +117,23 @@
 
 
 def prep_kernel(
-    rows, loops_ref, turned_ref, loops16_ref, design16_ref, turned16_ref, six_ref, direct_ref,
+    rows, loops_ref, turned_ref, both16_ref, design16_ref, six_ref, direct_ref,
     tall_ref, power_ref, total_ref, left_ref, right_ref,
 ):
     peers = tall_ref.shape[0] // rows
-    for source, wide, tall in ((loops_ref, loops16_ref, None), (turned_ref, turned16_ref, design16_ref)):
+    n = turned_ref.shape[0]
+    for source, base, tall in ((loops_ref, n, None), (turned_ref, 0, design16_ref)):
         for start in range(0, source.shape[0], LANES):
             size = min(LANES, source.shape[0] - start)
             tall_ref[:, :size] = source[start : start + size, :].astype(f32).T
             for r in range(rows):
                 some = tall_ref[pl.ds(r, peers, stride=rows), :]
-                wide[start : start + size, r * peers : (r + 1) * peers] = some.T[:size].astype(bf16)
+                both16_ref[base + start : base + start + size, r * peers : (r + 1) * peers] = some.T[:size].astype(bf16)
                 if tall is not None:
                     tall[r * peers : (r + 1) * peers, start : start + size] = some[:, :size].astype(bf16)
-    eye = eye_mask(turned_ref.shape[0])
-    gram = jnp.dot(turned16_ref[...], design16_ref[...], preferred_element_type=f32)
+    eye = eye_mask(n)
+    turned16 = both16_ref[:n, :]
+    gram = jnp.dot(turned16, design16_ref[...], preferred_element_type=f32)
     on_diagonal = jnp.where(eye, gram + ridge_weight, 0.0)
     column = jnp.sum(on_diagonal, axis=1, keepdims=True)
     row = jnp.sum(on_diagonal, axis=0, keepdims=True)
@@ -147,10 +149,9 @@
 
     lax.while_loop(lambda size: size > 3e-8, double, norm())
     pieces = thirds(total_ref[...] / row)
-    n = total_ref.shape[0]
     for k, (i, _) in enumerate(PAIRS):
         six_ref[:, k * n : (k + 1) * n] = pieces[i]
-    direct_ref[...] = sum(jnp.dot(p, turned16_ref[...], preferred_element_type=f32) for p in reversed(pieces))
+    direct_ref[...] = sum(jnp.dot(p, both16_ref[:n, :], preferred_element_type=f32) for p in reversed(pieces))
 
 
 def prep(loops, design, rows):
@@ -159,11 +160,10 @@
     return pl.pallas_call(
         functools.partial(prep_kernel, rows),
         in_specs=[VMEM, VMEM],
-        out_specs=[VMEM] * 5,
+        out_specs=[VMEM] * 4,
         out_shape=[
-            pltpu.HBM((n, m), bf16),
+            pltpu.HBM((dates + n, m), bf16),
             pltpu.HBM((m, dates), bf16),
-            pltpu.HBM((dates, m), bf16),
             pltpu.HBM((dates, dates * len(PAIRS)), bf16),
             pltpu.HBM((dates, m), f32),
         ],
@@ -186,83 +186,65 @@
     )
 
 
-def dates_kernel(
-    parts, rows, peers, held_ref, mine_ref, other_ref, turned_hbm, six_hbm, design_hbm, shifts_ref, line_ref,
-    turned_ref, six_ref, design_ref, wide_ref, stack_ref, sems,
+def main_kernel(
+    parts, rows, peers, held_ref, mine_ref, other_ref, both_hbm, six_hbm, design_hbm, shifts_ref, line_ref, closure_hbm,
+    both_ref, six_ref, design_ref, wide_ref, stack_ref, closure_ref, sems,
 ):
-    copies = [
-        pltpu.make_async_copy(turned_hbm, turned_ref, sems.at[0]),
-        pltpu.make_async_copy(six_hbm, six_ref, sems.at[1]),
-        pltpu.make_async_copy(design_hbm, design_ref, sems.at[2]),
-    ]
-    for copy in copies:
-        copy.start()
+    pairs = ((both_hbm, both_ref), (six_hbm, six_ref), (design_hbm, design_ref))
+    copies = [pltpu.make_async_copy(a, b, sems.at[k]) for k, (a, b) in enumerate(pairs)]
+    copies[0].start()
     for r in range(rows):
         side_by_side(wide_ref, slice(r * peers, (r + 1) * peers), lines_of(held_ref, r, parts, peers))
     copies[0].wait()
-    projected = folded(jnp.dot(turned_ref[...], wide_ref[...], preferred_element_type=f32), 3)
-    stack_right(stack_ref, projected)
+    copies[1].start()
+    copies[2].start()
+    products = folded(jnp.dot(both_ref[...], wide_ref[...], preferred_element_type=f32), 3)
+    dates = shifts_ref.shape[0]
+    closure_ref[...] = products[dates:]
+    copies.append(pltpu.make_async_copy(closure_ref, closure_hbm.at[0], sems.at[3]))
+    copies[3].start()
+    stack_right(stack_ref, products[:dates])
     copies[1].wait()
     shifts = jnp.dot(six_ref[...], stack_ref[...], preferred_element_type=f32)
     shifts_ref[...] = shifts
     two = jnp.concatenate(thirds(shifts)[:2], axis=1)
     copies[2].wait()
+    model = folded(jnp.dot(design_ref[...], two, preferred_element_type=f32), 2)
     square = 0.0
     for r in range(rows):
-        model = folded(jnp.dot(design_ref[r * peers : (r + 1) * peers, :], two, preferred_element_type=f32), 2)
-        residual = lines_of(held_ref, r, parts, peers) - model
+        residual = lines_of(held_ref, r, parts, peers) - model[r * peers : (r + 1) * peers]
         square += jnp.sum((residual * residual).reshape(peers // 8, 8, parts * LANES), axis=0)
     lane = lax.broadcasted_iota(jnp.int32, (1, LANES), 1)
     line = jnp.where(lane == 0, jnp.sum(square, keepdims=True), mine_ref[:1] + other_ref[:1])
     line_ref[...] = jnp.broadcast_to(line, line_ref.shape)
-
-
-def dates_part(c, turned16, mine, other, design16, six, parts, rows, peers):
+    copies[3].wait()
+
+
+def main_part(c, mine, other, both16, six, design16, parts, rows, peers):
     ifgs, dates = design16.shape
-    return pl.pallas_call(
-        functools.partial(dates_kernel, parts, rows, peers),
+    pixels = parts * LANES
+    n = both16.shape[0] - dates
+    return pl.pallas_call(
+        functools.partial(main_kernel, parts, rows, peers),
         in_specs=[VMEM] * 3 + [HBM] * 3,
-        out_specs=[VMEM] * 2,
+        out_specs=[VMEM, VMEM, HBM],
         out_shape=[
-            jax.ShapeDtypeStruct((dates, parts * LANES), f32),
-            pltpu.HBM((peers, LANES), f32),
+            jax.ShapeDtypeStruct((dates, pixels), f32),
+            jax.ShapeDtypeStruct((peers, LANES), f32),
+            pltpu.HBM((1, n, pixels), f32),
         ],
         scratch_shapes=[
-            pltpu.VMEM(turned16.shape, bf16),
+            pltpu.VMEM(both16.shape, bf16),
             pltpu.VMEM(six.shape, bf16),
             pltpu.VMEM(design16.shape, bf16),
-            pltpu.VMEM((ifgs, 3 * parts * LANES), bf16),
-            pltpu.VMEM((dates * len(PAIRS), parts * LANES), bf16),
-            pltpu.SemaphoreType.DMA((3,)),
-        ],
-        compiler_params=SMALL,
-        name="dates",
-    )(c, mine, other, in_hbm(turned16), in_hbm(six), in_hbm(design16))
-
-
-def loops_kernel(parts, rows, peers, held_ref, loops_hbm, closure_ref, loops_ref, wide_ref, sem):
-    copy = pltpu.make_async_copy(loops_hbm, loops_ref, sem)
-    copy.start()
-    for r in range(rows):
-        side_by_side(wide_ref, slice(r * peers, (r + 1) * peers), lines_of(held_ref, r, parts, peers))
-    copy.wait()
-    closure_ref[0] = folded(jnp.dot(loops_ref[...], wide_ref[...], preferred_element_type=f32), 3)
-
-
-def loops_part(c, loops16, parts, rows, peers):
-    return pl.pallas_call(
-        functools.partial(loops_kernel, parts, rows, peers),
-        in_specs=[VMEM, HBM],
-        out_specs=VMEM,
-        out_shape=jax.ShapeDtypeStruct((1, loops16.shape[0], parts * LANES), f32),
-        scratch_shapes=[
-            pltpu.VMEM(loops16.shape, bf16),
-            pltpu.VMEM((loops16.shape[1], 3 * parts * LANES), bf16),
-            pltpu.SemaphoreType.DMA,
-        ],
-        compiler_params=SMALL,
-        name="loops",
-    )(c, in_hbm(loops16))
+            pltpu.VMEM((ifgs, 3 * pixels), bf16),
+            pltpu.VMEM((dates * len(PAIRS), pixels), bf16),
+            pltpu.VMEM((n, pixels), f32),
+            pltpu.SemaphoreType.DMA((4,)),
+        ],
+        compiler_params=pltpu.CompilerParams(vmem_limit_bytes=28 * 2**20),
+        name="main",
+    )(c, mine, other, in_hbm(both16), in_hbm(six), in_hbm(design16))
 
 
 def last_kernel(rows, count, squares, got_ref, direct_ref, shifts_ref, displacement_ref, misfit_ref):
@@ -298,10 +280,9 @@
     got = lax.all_to_all(tiles.reshape(peers, 1, -1), IFG, split_axis=0, concat_axis=0, tiled=True)
     got = got.reshape(tiles.shape)
     other = lax.ppermute(mine, "slab", [(i, (i + 1) % slabs) for i in range(slabs)])
-    loops16, design16, turned16, six, direct = prep(closure_loops, design, rows)
-    shifts, line = dates_part(got, turned16, mine, other, design16, six, parts, rows, peers)
+    both16, design16, six, direct = prep(closure_loops, design, rows)
+    shifts, line, closure = main_part(got, mine, other, both16, six, design16, parts, rows, peers)
     totals = lax.all_to_all(line.reshape(peers, 1, LANES), IFG, split_axis=0, concat_axis=0, tiled=True)
-    closure = loops_part(got, loops16, parts, rows, peers)
     displacement, misfit = last_part(
         totals.reshape(peers, LANES), direct, shifts, rows, slabs * pixels, design.shape[0] * pixels
     )

time: 87.6 us -> 86 us (0.982)
  blocking collectives: 0 us -> 15.7 us
  starting transfers between devices: 25.8 us -> 18.3 us
  waiting for transfers between devices: 28.4 us -> 21.5 us
  Pallas kernels: 31 us -> 28.3 us
    all_to_all x0 -> x1, blocking collectives: none -> 15.7 us  [local(): lax.all_to_all(line.reshape(peers, 1, LANES), IFG, split_axis=0, concat_a...]
    all_to_all x1 -> x0, starting transfers between devices: 7.53 us -> none  [local(): lax.all_to_all(line.reshape(peers, 1, LANES), IFG, split_axis=0, concat_a...]
    all_to_all x1 -> x0, waiting for transfers between devices: 6.88 us -> none  [local(): lax.all_to_all(line.reshape(peers, 1, LANES), IFG, split_axis=0, concat_a...]
    pallas_call x2 -> x1, Pallas kernels: 7.94 us -> 6.01 us  [main_part(): pl.pallas_call(functools.partial(main_kernel, parts, rows, peers), in_spe...]
  transfers between devices with their start and end apart: 3 -> 2, of which waited for: 3 -> 2; matrix products, arithmetic and copies ran while one was open for 0% -> 0% of each run, Pallas kernels for 24% -> 21%
where the time goes in v3:
time: 86 us; the launch traced here: 85.7 us
  Pallas kernels  28.3 us (33%)
  waiting for transfers between devices  21.5 us (25%)
  starting transfers between devices  18.3 us (21%)
  blocking collectives  15.7 us (18%)
  local copies, waits for them, and re-layouts  1.34 us (2%)
    pallas_call x1, Pallas kernels, prep(): pl.pallas_call(functools.partial(prep_kernel, rows), in_specs=[VMEM, VMEM...  18 us
    all_to_all x1, blocking collectives, local(): lax.all_to_all(line.reshape(peers, 1, LANES), IFG, split_axis=0, concat_a...  15.7 us
    all_to_all x1, starting transfers between devices, local(): lax.all_to_all(tiles.reshape(peers, 1, -1), IFG, split_axis=0, concat_axi...  14 us
    all_to_all x1, waiting for transfers between devices, local(): lax.all_to_all(tiles.reshape(peers, 1, -1), IFG, split_axis=0, concat_axi...  12.6 us
    ppermute x1, waiting for transfers between devices, local(): lax.ppermute(mine, 'slab', [(i, (i + 1) % slabs) for i in range(slabs)])  8.87 us
    pallas_call x1, Pallas kernels, main_part(): pl.pallas_call(functools.partial(main_kernel, parts, rows, peers), in_spe...  6.01 us
    ppermute x1, starting transfers between devices, local(): lax.ppermute(mine, 'slab', [(i, (i + 1) % slabs) for i in range(slabs)])  4.3 us
    pallas_call x1, Pallas kernels, head(): pl.pallas_call(functools.partial(head_kernel, parts, chunks), in_specs=[H...  3.32 us
  transfers between devices with their start and end apart: 2, of which 2 were waited for; matrix products, arithmetic and copies ran while one was open for 0% of the time, Pallas kernels for 21%

profile of v3, /device:TPU:1, one launch (start us, length us, event | category | flops | bytes accessed | tf_op | source)
XLA Modules:
  0.0 85.7 jit_solution(10673623203705295265)
XLA Ops:
  0.6 3.3 %head.1 = (f32[3456,128]{1,0:T(8,128)}, f32[8,128]{1,0:T(8,128)}) custom-call(f32[9,384,128]{2,1,0:T(8,128)} %bitcast.15, s32[9,384,128]{2,1,0:T(8,128)} %bitcast.16), custom_call_target="tpu_custom_call" | custom-call | tf_op jit(solution)/shard_map/head/pallas_call | solution.py:87
  4.0 0.0 copy-start.3
  4.0 0.0 copy-start.1
  4.0 14.0 %all-to-all-start = ((f32[128,1,3456]{2,1,0:T(1,128)}), f32[128,1,3456]{2,1,0:T(1,128)S(1)}, u32[]{:S(2)}, u32[]{:S(2)}) async-start(f32[128,1,3456]{2,1,0:T(1,128)} %bitcast.17), calls=%async_computation | async-start | bytes 3538944 | tf_op jit(solution)/shard_map/all_to_all | solution.py:280
  18.0 0.0 copy-done.3
  18.0 4.3 %collective-permute-start = (f32[8,128]{1,0:T(8,128)S(1)}, f32[8,128]{1,0:T(8,128)S(1)}, u32[]{:S(2)}, u32[]{:S(2)}) collective-permute-start(f32[8,128]{1,0:T(8,128)S(1)} %copy-done.3), channel_id=1, source_target_pairs={{0,1},{1,0},{2,3},{3,2},{4,5},{5,4},{6,7},{7,6},{8,9},{9,8},{10,11... | collective-permute-start | bytes 12296 | tf_op jit(solution)/shard_map/ppermute | solution.py:282
  22.3 0.0 copy-done.1
  22.3 0.0 copy-start.2
  22.3 1.3 %copy-done.2 = s32[1152,288]{0,1:T(8,128)S(1)} copy-done((s32[1152,288]{0,1:T(8,128)S(1)}, s32[1152,288]{0,1:T(8,128)}, u32[]{:S(2)}) %copy-start.2) | copy-done | bytes 1327128
  23.6 18.0 %prep.1 = (bf16[576,1152]{1,0:T(8,128)(2,1)}, bf16[1152,288]{1,0:T(8,128)(2,1)}, bf16[288,1728]{1,0:T(8,128)(2,1)}, f32[288,1152]{1,0:T(8,128)}) custom-call(s32[288,1152]{1,0:T(8,128)S(1)} %copy-done.1, s32[288,1152]{1,0:T(8,128)S(1)} %bitcast.12), custom_call_target="tpu_custom_call" | custom-call | tf_op jit(solution)/shard_map/prep/pallas_call | solution.py:160
  41.5 8.9 %collective-permute-done.other_ref = f32[8,128]{1,0:T(8,128)S(1)} collective-permute-done((f32[8,128]{1,0:T(8,128)S(1)}, f32[8,128]{1,0:T(8,128)S(1)}, u32[]{:S(2)}, u32[]{:S(2)}) %collective-permute-start) | collective-permute-done | bytes 4128 | tf_op jit(solution)/shard_map/ppermute | solution.py:282
  50.4 12.6 %all-to-all-done = f32[128,1,3456]{2,1,0:T(1,128)S(1)} async-done(((f32[128,1,3456]{2,1,0:T(1,128)}), f32[128,1,3456]{2,1,0:T(1,128)S(1)}, u32[]{:S(2)}, u32[]{:S(2)}) %all-to-all-start) | async-done | bytes 1769504 | tf_op jit(solution)/shard_map/all_to_all | solution.py:280
  63.0 0.0 copy-start
  63.0 6.0 %main.1 = (f32[288,384]{1,0:T(8,128)S(1)}, f32[128,128]{1,0:T(8,128)S(1)}, f32[1,288,384]{2,1,0:T(8,128)}) custom-call(f32[3456,128]{1,0:T(8,128)S(1)} %bitcast.11, f32[8,128]{1,0:T(8,128)S(1)} %copy-done.3, f32[8,128]{1,0:T(8,128)S(1)} %collective-permute-done.other_ref, bf16[576,1152]{1,0:T(8,128)(2,1)} %get-tuple-element.16.both_hbm, ...), custom_call_target="tpu_custom_call" | custom-call | tf_op jit(solution)/shard_map/main/pallas_call | solution.py:227
  69.0 15.7 %all_to_all.10 = f32[128,1,128]{2,1,0:T(1,128)S(1)} all-to-all(f32[128,1,128]{2,1,0:T(1,128)S(1)} %bitcast.14), channel_id=1, replica_groups=mesh['ifg_0'=4,'ifg_1'=4,'ifg_2'=4,'ifg_3'=2,'slab'=2] {'ifg_0','ifg_1',..., dimensions={0} | all-to-all | bytes 131072 | tf_op jit(solution)/shard_map/all_to_all | solution.py:285
  84.7 0.0 copy-done
  84.7 1.0 %last.1 = (f32[1,288,384]{2,1,0:T(8,128)}, f32[1,128]{1,0:T(1,128)}) custom-call(f32[128,128]{1,0:T(8,128)S(1)} %bitcast.13, f32[288,1152]{1,0:T(8,128)S(1)} %copy-done, f32[288,384]{1,0:T(8,128)S(1)} %get-tuple-element.22.shifts_ref), custom_call_target="tpu_custom_call" | custom-call | tf_op jit(solution)/shard_map/last/pallas_call | solution.py:260
Async XLA Ops:
  4.0 14.0 %copy-start.3 = (f32[8,128]{1,0:T(8,128)S(1)}, f32[8,128]{1,0:T(8,128)}, u32[]{:S(2)}) copy-start(f32[8,128]{1,0:T(8,128)} %get-tuple-element.15.mine_ref) | copy-start | bytes 12292
  4.0 18.3 %copy-start.1 = (s32[288,1152]{1,0:T(8,128)S(1)}, s32[288,1152]{1,0:T(8,128)}, u32[]{:S(2)}) copy-start(s32[288,1152]{1,0:T(8,128)} %loops_ref.1) | copy-start | bytes 3981316
  4.0 59.0 %all-to-all-start = ((f32[128,1,3456]{2,1,0:T(1,128)}), f32[128,1,3456]{2,1,0:T(1,128)S(1)}, u32[]{:S(2)}, u32[]{:S(2)}) async-start(f32[128,1,3456]{2,1,0:T(1,128)} %bitcast.17), calls=%async_computation | async-start | bytes 3538944 | tf_op jit(solution)/shard_map/all_to_all | solution.py:280
  18.0 32.5 %collective-permute-start = (f32[8,128]{1,0:T(8,128)S(1)}, f32[8,128]{1,0:T(8,128)S(1)}, u32[]{:S(2)}, u32[]{:S(2)}) collective-permute-start(f32[8,128]{1,0:T(8,128)S(1)} %copy-done.3), channel_id=1, source_target_pairs={{0,1},{1,0},{2,3},{3,2},{4,5},{5,4},{6,7},{7,6},{8,9},{9,8},{10,11... | collective-permute-start | bytes 12296 | tf_op jit(solution)/shard_map/ppermute | solution.py:282
  22.3 1.3 %copy-start.2 = (s32[1152,288]{0,1:T(8,128)S(1)}, s32[1152,288]{0,1:T(8,128)}, u32[]{:S(2)}) copy-start(s32[1152,288]{0,1:T(8,128)} %param.7) | copy-start | bytes 3981316
  63.0 21.7 %copy-start = (f32[288,1152]{1,0:T(8,128)S(1)}, f32[288,1152]{1,0:T(8,128)}, u32[]{:S(2)}) copy-start(f32[288,1152]{1,0:T(8,128)} %get-tuple-element.21.direct_ref) | copy-start | bytes 3981316

commit v4 on v3

--- a/solution.py
+++ b/solution.py
@@ -54,7 +54,7 @@
     return sum(wide[:, k * n : (k + 1) * n] for k in reversed(range(count)))
 
 
-def head_kernel(parts, chunks, phase_ref, counts_ref, out_ref, sums_ref, phase_in, counts_in, sems):
+def head_kernel(parts, chunks, phase_ref, counts_ref, out_ref, phase_in, counts_in, sems):
     rows, lines, _ = phase_ref.shape
     peers = lines // parts
     span, group = lines // chunks, peers // chunks
@@ -65,7 +65,6 @@
         for s, (a, b) in enumerate(((phase_ref, phase_in), (counts_ref, counts_in))):
             copies.append(pltpu.make_async_copy(a.at[:, at, :], b.at[:, at, :], sems.at[k, s]))
             copies[-1].start()
-    sums = [jnp.zeros((8, LANES), f32) for _ in range(rows)]
     for k in range(chunks):
         copies[2 * k].wait()
         copies[2 * k + 1].wait()
@@ -74,12 +73,6 @@
                 at = pl.ds(k * span + j, group, stride=parts)
                 some = phase_in[r, at, :] + two_pi * counts_in[r, at, :].astype(f32)
                 out_ref[pl.ds(k * group * pitch + r * parts + j, group, stride=pitch), :] = some
-                sums[r] += jnp.sum(some.reshape(group // 8, 8, LANES), axis=0)
-    lane = lax.broadcasted_iota(jnp.int32, (1, LANES), 1)
-    total = jnp.zeros((1, LANES), f32)
-    for r in range(rows):
-        total = jnp.where(lane == r + 1, jnp.sum(sums[r], keepdims=True), total)
-    sums_ref[...] = jnp.broadcast_to(total, sums_ref.shape)
 
 
 def head(phase, counts, parts, chunks):
@@ -87,8 +80,8 @@
     return pl.pallas_call(
         functools.partial(head_kernel, parts, chunks),
         in_specs=[HBM, HBM],
-        out_specs=[VMEM, VMEM],
-        out_shape=[pltpu.HBM((lines * rows, LANES), f32), jax.ShapeDtypeStruct((8, LANES), f32)],
+        out_specs=VMEM,
+        out_shape=pltpu.HBM((lines * rows, LANES), f32),
         scratch_shapes=[
             pltpu.VMEM(phase.shape, f32),
             pltpu.VMEM(phase.shape, jnp.int32),
@@ -96,6 +89,29 @@
         ],
         name="head",
     )(in_hbm(phase), in_hbm(counts))
+
+
+def sums_kernel(rows, parts, peers, tiles_ref, sums_ref):
+    pitch = rows * parts
+    lane = lax.broadcasted_iota(jnp.int32, (1, LANES), 1)
+    total = jnp.zeros((1, LANES), f32)
+    for r in range(rows):
+        row = 0.0
+        for j in range(parts):
+            some = tiles_ref[pl.ds(r * parts + j, peers, stride=pitch), :]
+            row += jnp.sum(some.reshape(peers // 8, 8, LANES), axis=0)
+        total = jnp.where(lane == r + 1, jnp.sum(row, keepdims=True), total)
+    sums_ref[...] = jnp.broadcast_to(total, sums_ref.shape)
+
+
+def sums_part(tiles, rows, parts, peers):
+    return pl.pallas_call(
+        functools.partial(sums_kernel, rows, parts, peers),
+        in_specs=[VMEM],
+        out_specs=VMEM,
+        out_shape=jax.ShapeDtypeStruct((8, LANES), f32),
+        name="sums",
+    )(in_hbm(tiles))
 
 
 def eye_mask(n):
@@ -276,9 +292,10 @@
     rows, pixels = phase.shape[1:]
     parts = pixels // (peers * LANES)
     lines = (rows, pixels // LANES, LANES)
-    tiles, mine = head(phase.reshape(lines), corrections.reshape(lines), parts, 4)
+    tiles = head(phase.reshape(lines), corrections.reshape(lines), parts, 4)
     got = lax.all_to_all(tiles.reshape(peers, 1, -1), IFG, split_axis=0, concat_axis=0, tiled=True)
     got = got.reshape(tiles.shape)
+    mine = sums_part(tiles, rows, parts, peers)
     other = lax.ppermute(mine, "slab", [(i, (i + 1) % slabs) for i in range(slabs)])
     both16, design16, six, direct = prep(closure_loops, design, rows)
     shifts, line, closure = main_part(got, mine, other, both16, six, design16, parts, rows, peers)

time: 86 us -> 85.9 us (level)
  Pallas kernels: 28.3 us -> 30.7 us
  waiting for transfers between devices: 21.5 us -> 19.2 us
    pallas_call x0 -> x1, Pallas kernels: none -> 2.38 us  [sums_part(): pl.pallas_call(functools.partial(sums_kernel, rows, parts, peers), in_spe...]
    ppermute x1, waiting for transfers between devices: 8.87 us -> 6.6 us  [local(): lax.ppermute(mine, 'slab', [(i, (i + 1) % slabs) for i in range(slabs)])]
  transfers between devices with their start and end apart: 2 -> 2, of which waited for: 2 -> 2; matrix products, arithmetic and copies ran while one was open for 0% -> 0% of each run, Pallas kernels for 21% -> 24%
where the time goes in v4:
time: 85.9 us; the launch traced here: 85.6 us
  Pallas kernels  30.7 us (36%)
  waiting for transfers between devices  19.2 us (22%)
  starting transfers between devices  18 us (21%)
  blocking collectives  15.7 us (18%)
  local copies, waits for them, and re-layouts  1.34 us (2%)
    pallas_call x1, Pallas kernels, prep(): pl.pallas_call(functools.partial(prep_kernel, rows), in_specs=[VMEM, VMEM...  17.9 us
    all_to_all x1, blocking collectives, local(): lax.all_to_all(line.reshape(peers, 1, LANES), IFG, split_axis=0, concat_a...  15.7 us
    all_to_all x1, starting transfers between devices, local(): lax.all_to_all(tiles.reshape(peers, 1, -1), IFG, split_axis=0, concat_axi...  13.8 us
    all_to_all x1, waiting for transfers between devices, local(): lax.all_to_all(tiles.reshape(peers, 1, -1), IFG, split_axis=0, concat_axi...  12.6 us
    ppermute x1, waiting for transfers between devices, local(): lax.ppermute(mine, 'slab', [(i, (i + 1) % slabs) for i in range(slabs)])  6.6 us
    pallas_call x1, Pallas kernels, main_part(): pl.pallas_call(functools.partial(main_kernel, parts, rows, peers), in_spe...  6.02 us
    ppermute x1, starting transfers between devices, local(): lax.ppermute(mine, 'slab', [(i, (i + 1) % slabs) for i in range(slabs)])  4.21 us
    pallas_call x1, Pallas kernels, head(): pl.pallas_call(functools.partial(head_kernel, parts, chunks), in_specs=[H...  3.32 us
  transfers between devices with their start and end apart: 2, of which 2 were waited for; matrix products, arithmetic and copies ran while one was open for 0% of the time, Pallas kernels for 24%

profile of v4, /device:TPU:1, one launch (start us, length us, event | category | flops | bytes accessed | tf_op | source)
XLA Modules:
  0.0 85.6 jit_solution(12436929993993406741)
XLA Ops:
  0.6 3.3 %head.1.tiles_ref = f32[3456,128]{1,0:T(8,128)} custom-call(f32[9,384,128]{2,1,0:T(8,128)} %bitcast.16, s32[9,384,128]{2,1,0:T(8,128)} %bitcast.17), custom_call_target="tpu_custom_call" | custom-call | tf_op jit(solution)/shard_map/head/pallas_call | solution.py:80
  4.0 13.8 %all-to-all-start = ((f32[128,1,3456]{2,1,0:T(1,128)}), f32[128,1,3456]{2,1,0:T(1,128)S(1)}, u32[]{:S(2)}, u32[]{:S(2)}) async-start(f32[128,1,3456]{2,1,0:T(1,128)} %bitcast.15), calls=%async_computation | async-start | bytes 3538944 | tf_op jit(solution)/shard_map/all_to_all | solution.py:296
  17.8 0.0 copy-start.1
  17.8 2.4 %sums.1.mine_ref = f32[8,128]{1,0:T(8,128)} custom-call(f32[3456,128]{1,0:T(8,128)} %head.1.tiles_ref), custom_call_target="tpu_custom_call" | custom-call | tf_op jit(solution)/shard_map/sums/pallas_call | solution.py:108
  20.2 4.2 %collective-permute-start = (f32[8,128]{1,0:T(8,128)}, f32[8,128]{1,0:T(8,128)S(1)}, u32[]{:S(2)}, u32[]{:S(2)}) collective-permute-start(f32[8,128]{1,0:T(8,128)} %sums.1.mine_ref), channel_id=1, source_target_pairs={{0,1},{1,0},{2,3},{3,2},{4,5},{5,4},{6,7},{7,6},{8,9},{9,8},{10,11... | collective-permute-start | bytes 12296 | tf_op jit(solution)/shard_map/ppermute | solution.py:299
  24.4 0.0 copy-done.1
  24.4 0.0 copy-start.2
  24.4 1.3 %copy-done.2 = s32[1152,288]{0,1:T(8,128)S(1)} copy-done((s32[1152,288]{0,1:T(8,128)S(1)}, s32[1152,288]{0,1:T(8,128)}, u32[]{:S(2)}) %copy-start.2) | copy-done | bytes 1327128
  25.7 0.0 copy-start.3
  25.7 17.9 %prep.1 = (bf16[576,1152]{1,0:T(8,128)(2,1)}, bf16[1152,288]{1,0:T(8,128)(2,1)}, bf16[288,1728]{1,0:T(8,128)(2,1)}, f32[288,1152]{1,0:T(8,128)}) custom-call(s32[288,1152]{1,0:T(8,128)S(1)} %copy-done.1, s32[288,1152]{1,0:T(8,128)S(1)} %bitcast.12), custom_call_target="tpu_custom_call" | custom-call | tf_op jit(solution)/shard_map/prep/pallas_call | solution.py:176
  43.7 6.6 %collective-permute-done.other_ref = f32[8,128]{1,0:T(8,128)S(1)} collective-permute-done((f32[8,128]{1,0:T(8,128)}, f32[8,128]{1,0:T(8,128)S(1)}, u32[]{:S(2)}, u32[]{:S(2)}) %collective-permute-start) | collective-permute-done | bytes 4128 | tf_op jit(solution)/shard_map/ppermute | solution.py:299
  50.3 12.6 %all-to-all-done = f32[128,1,3456]{2,1,0:T(1,128)S(1)} async-done(((f32[128,1,3456]{2,1,0:T(1,128)}), f32[128,1,3456]{2,1,0:T(1,128)S(1)}, u32[]{:S(2)}, u32[]{:S(2)}) %all-to-all-start) | async-done | bytes 1769504 | tf_op jit(solution)/shard_map/all_to_all | solution.py:296
  62.9 0.0 copy-done.3
  62.9 0.0 copy-start
  62.9 6.0 %main.1 = (f32[288,384]{1,0:T(8,128)S(1)}, f32[128,128]{1,0:T(8,128)S(1)}, f32[1,288,384]{2,1,0:T(8,128)}) custom-call(f32[3456,128]{1,0:T(8,128)S(1)} %bitcast.11, f32[8,128]{1,0:T(8,128)S(1)} %copy-done.3, f32[8,128]{1,0:T(8,128)S(1)} %collective-permute-done.other_ref, bf16[576,1152]{1,0:T(8,128)(2,1)} %get-tuple-element.12.both_hbm, ...), custom_call_target="tpu_custom_call" | custom-call | tf_op jit(solution)/shard_map/main/pallas_call | solution.py:243
  68.9 15.7 %all_to_all.10 = f32[128,1,128]{2,1,0:T(1,128)S(1)} all-to-all(f32[128,1,128]{2,1,0:T(1,128)S(1)} %bitcast.14), channel_id=1, replica_groups=mesh['ifg_0'=4,'ifg_1'=4,'ifg_2'=4,'ifg_3'=2,'slab'=2] {'ifg_0','ifg_1',..., dimensions={0} | all-to-all | bytes 131072 | tf_op jit(solution)/shard_map/all_to_all | solution.py:302
  84.6 0.0 copy-done
  84.6 1.0 %last.1 = (f32[1,288,384]{2,1,0:T(8,128)}, f32[1,128]{1,0:T(1,128)}) custom-call(f32[128,128]{1,0:T(8,128)S(1)} %bitcast.13, f32[288,1152]{1,0:T(8,128)S(1)} %copy-done, f32[288,384]{1,0:T(8,128)S(1)} %get-tuple-element.18.shifts_ref), custom_call_target="tpu_custom_call" | custom-call | tf_op jit(solution)/shard_map/last/pallas_call | solution.py:276
Async XLA Ops:
  4.0 58.9 %all-to-all-start = ((f32[128,1,3456]{2,1,0:T(1,128)}), f32[128,1,3456]{2,1,0:T(1,128)S(1)}, u32[]{:S(2)}, u32[]{:S(2)}) async-start(f32[128,1,3456]{2,1,0:T(1,128)} %bitcast.15), calls=%async_computation | async-start | bytes 3538944 | tf_op jit(solution)/shard_map/all_to_all | solution.py:296
  17.8 6.6 %copy-start.1 = (s32[288,1152]{1,0:T(8,128)S(1)}, s32[288,1152]{1,0:T(8,128)}, u32[]{:S(2)}) copy-start(s32[288,1152]{1,0:T(8,128)} %loops_ref.1) | copy-start | bytes 3981316
  20.2 30.1 %collective-permute-start = (f32[8,128]{1,0:T(8,128)}, f32[8,128]{1,0:T(8,128)S(1)}, u32[]{:S(2)}, u32[]{:S(2)}) collective-permute-start(f32[8,128]{1,0:T(8,128)} %sums.1.mine_ref), channel_id=1, source_target_pairs={{0,1},{1,0},{2,3},{3,2},{4,5},{5,4},{6,7},{7,6},{8,9},{9,8},{10,11... | collective-permute-start | bytes 12296 | tf_op jit(solution)/shard_map/ppermute | solution.py:299
  24.4 1.3 %copy-start.2 = (s32[1152,288]{0,1:T(8,128)S(1)}, s32[1152,288]{0,1:T(8,128)}, u32[]{:S(2)}) copy-start(s32[1152,288]{0,1:T(8,128)} %param.7) | copy-start | bytes 3981316
  25.7 37.1 %copy-start.3 = (f32[8,128]{1,0:T(8,128)S(1)}, f32[8,128]{1,0:T(8,128)}, u32[]{:S(2)}) copy-start(f32[8,128]{1,0:T(8,128)} %sums.1.mine_ref) | copy-start | bytes 12292
  62.9 21.7 %copy-start = (f32[288,1152]{1,0:T(8,128)S(1)}, f32[288,1152]{1,0:T(8,128)}, u32[]{:S(2)}) copy-start(f32[288,1152]{1,0:T(8,128)} %get-tuple-element.17.direct_ref) | copy-start | bytes 3981316
